TPU v7x, 32 devices: a whole 2x2x4 slice. The times are simulated.
32 devices in a mesh: af: 4 (over z), gx: 2 (over x), gy: 4 (over y, core).
Axes of the slice: x: 2, y: 2, z: 4, core: 2. Of those that a mesh axis runs over, the one named last changes fastest.
Arguments:
- source: float32 [4, 2048, 2048], P('af', ('gx', 'gy')), parts along dimension 0, may hold values from -0.8 to 0.8
- screening: float32 [4], P('af'), parts along dimension 0, may hold values from 0.0002 to 0.002
Outputs:
- solution: float32 [4, 2048, 2048], P('af', ('gx', 'gy')), parts along dimension 0
There are 4 independent parts, one for each index of `af`. A program takes and returns all parts, laid end to end along the dimension named above; each array names one. Nothing has to cross between parts.
All inputs are finite; a program needn't handle non-finite values.
Results may differ from a plain program's by a relative error of at most 0.0014.
Values sent between devices are 32-bit elements; how exact they have to be, the bound alone decides.
A program may use at most 128 MiB of HBM per device.

v0:
```python
import functools
import math

import jax
import jax.numpy as jnp
import numpy as np
from jax import lax
from jax.experimental import pallas as pl
from jax.experimental.pallas import tpu as pltpu
from jax.sharding import PartitionSpec as P

LANES = 128
SEGMENTS = 8
TILE = 256
STEP = 32
GRID_AXES = ("gx", "gy")
MESH = pl.DeviceIdType.MESH


def mode_numbers(length):
    half = length // 2
    numbers = np.arange(half, dtype=np.int64) + 1
    return np.concatenate([2 * numbers, length + 1 - 2 * numbers])


def double_cosines(length):
    angles = mode_numbers(length).astype(np.float32) * np.float32(math.pi / (length + 1))
    return (np.float32(2.0) * np.cos(angles.astype(np.float64)).astype(np.float32))[None, :]


def angle_tables(length):
    half = length // 2
    columns = np.arange(half, dtype=np.int64)[None, :] + 1
    coarse = np.arange(half // STEP, dtype=np.int64)[:, None] * STEP
    fine = np.arange(STEP, dtype=np.int64)[:, None] + 1
    scale = math.sqrt(2.0 / (length + 1))
    angle = lambda rows: 2.0 * math.pi * (rows * columns % (length + 1)) / (length + 1)
    tables = (
        scale * np.sin(angle(coarse)),
        scale * np.cos(angle(coarse)),
        np.sin(angle(fine)),
        np.cos(angle(fine)),
    )
    return tuple(table.astype(np.float32) for table in tables)


def power(base, exponent):
    result = None
    while exponent:
        if exponent & 1:
            result = base if result is None else result * base
        exponent >>= 1
        if exponent:
            base = base * base
    return result


def decay_of(screening, cosines):
    factor = (4.0 + screening) - cosines
    excess = factor - 2.0
    root = jnp.sqrt(excess * (excess + 4.0))
    return 2.0 / (factor + root), root


def split(values):
    high = values.astype(jnp.bfloat16)
    return high, (values - high.astype(jnp.float32)).astype(jnp.bfloat16)


def mirrored(values):
    lanes = lax.broadcasted_iota(jnp.int32, values.shape, 1)
    return jnp.take_along_axis(values, LANES - 1 - lanes, axis=1)


def parity(shape):
    lanes = lax.broadcasted_iota(jnp.int32, shape, 1)
    return jnp.where(lanes % 2 == 0, 1.0, -1.0)


def table_tile(tables, table_high, table_low, columns):
    coarse_sin, coarse_cos, fine_sin, fine_cos = tables
    for a in range(coarse_sin.shape[0]):
        values = (
            coarse_sin[a : a + 1, columns] * fine_cos[:, columns]
            + coarse_cos[a : a + 1, columns] * fine_sin[:, columns]
        )
        high, low = split(values)
        table_high[a * STEP : (a + 1) * STEP, columns] = high
        table_low[a * STEP : (a + 1) * STEP, columns] = low


def product(high, low, table_high, table_low, columns):
    dot = functools.partial(jnp.dot, preferred_element_type=jnp.float32)
    return (
        dot(high[...], table_high[:, columns])
        + dot(low[...], table_high[:, columns])
        + dot(high[...], table_low[:, columns])
    )


def peer(index):
    across = lax.axis_size("gy")
    return {"gx": index // across, "gy": index % across}


def forward_kernel(
    groups, source, screening, cosines, coarse_sin, coarse_cos, fine_sin, fine_cos,
    spectrum, left_parts, right_parts, all_moments,
    high, low, table_high, table_low, stage, arrived,
    moments, landed, send_sems, recv_sems,
):
    tables = (coarse_sin, coarse_cos, fine_sin, fine_cos)
    rows, length = source.shape
    blocks = length // LANES
    copies = [
        pltpu.make_async_copy(source.at[:, pl.ds(c * LANES, LANES)], stage.at[c], arrived.at[c])
        for c in range(blocks)
    ]
    for copy in copies:
        copy.start()
    half = length // 2
    steps = rows // SEGMENTS
    position = lax.axis_index(GRID_AXES)
    barrier = pltpu.get_barrier_semaphore()
    for d in range(1, groups):
        pl.semaphore_signal(barrier, inc=1, device_id=peer((position + d) % groups), device_id_type=MESH)
    signs = parity((2 * SEGMENTS, LANES))
    for copy in copies:
        copy.wait()
    for c in range(blocks // 2):
        columns = pl.ds(c * LANES, LANES)
        for g in range(0, steps, 2):
            place = pl.ds(g * SEGMENTS, 2 * SEGMENTS)
            place_sum = pl.ds(rows + g * SEGMENTS, 2 * SEGMENTS)

            def load(column):
                pair = [stage[column, pl.ds(g + e, SEGMENTS, stride=steps), :] for e in range(2)]
                return jnp.concatenate(pair, axis=0)

            near = load(c)
            far = mirrored(load(blocks - 1 - c))
            high[place, columns], low[place, columns] = split(near - far)
            high[place_sum, columns], low[place_sum, columns] = split((near + far) * signs)
    for t in range(half // TILE):
        columns = pl.ds(t * TILE, TILE)
        table_tile(tables, table_high, table_low, columns)
        values = product(high, low, table_high, table_low, columns)
        spectrum[:, t * TILE : (t + 1) * TILE] = values[:rows]
        spectrum[:, half + t * TILE : half + (t + 1) * TILE] = values[rows:]
    decay, _ = decay_of(screening[0], cosines[...])
    stride = power(decay, steps)
    for t in range(length // TILE):
        columns = slice(t * TILE, (t + 1) * TILE)
        ratio = jnp.broadcast_to(decay[:, columns], (SEGMENTS, TILE))
        left = right = jnp.zeros((SEGMENTS, TILE), jnp.float32)
        for g in range(steps):
            mirror = steps - 1 - g
            left = ratio * left + spectrum[g * SEGMENTS : (g + 1) * SEGMENTS, columns]
            right = ratio * right + spectrum[mirror * SEGMENTS : (mirror + 1) * SEGMENTS, columns]
        left_parts[:, columns] = left
        right_parts[:, columns] = right
    left = right = jnp.zeros((1, length), jnp.float32)
    for s in range(SEGMENTS):
        left = stride * left + left_parts[s : s + 1, :]
        right = stride * right + right_parts[SEGMENTS - 1 - s : SEGMENTS - s, :]
    moments[0:1, :] = left
    moments[1:2, :] = right
    pl.semaphore_wait(barrier, groups - 1)
    sends = []
    for d in range(1, groups):
        send = pltpu.make_async_remote_copy(
            src_ref=moments,
            dst_ref=landed.at[position],
            send_sem=send_sems.at[d],
            recv_sem=recv_sems.at[position],
            device_id=peer((position + d) % groups),
            device_id_type=MESH,
        )
        send.start()
        sends.append(send)
    all_moments[position] = moments[...]
    for d in range(1, groups):
        origin = (position + groups - d) % groups
        pltpu.make_async_remote_copy(
            src_ref=moments,
            dst_ref=landed.at[origin],
            send_sem=send_sems.at[d],
            recv_sem=recv_sems.at[origin],
            device_id=peer(origin),
            device_id_type=MESH,
        ).wait_recv()
        all_moments[origin] = landed[origin]
    for send in sends:
        send.wait_send()


def backward_kernel(
    groups, spectrum, left_parts, right_parts, all_moments, screening, cosines,
    coarse_sin, coarse_cos, fine_sin, fine_cos,
    solved, high, low, table_high, table_low, left_states, right_states, stage, stored,
):
    tables = (coarse_sin, coarse_cos, fine_sin, fine_cos)
    rows, length = spectrum.shape
    half = length // 2
    steps = rows // SEGMENTS
    position = lax.axis_index(GRID_AXES)
    decay, root = decay_of(screening[0], cosines[...])
    stride = power(decay, steps)
    block = power(decay, rows)
    whole = power(decay, rows * groups + 1)
    left_total = right_total = jnp.zeros((1, length), jnp.float32)
    for d in range(groups):
        left_total = block * left_total + all_moments[d, 0:1, :]
        e = groups - 1 - d
        right_total = block * right_total + all_moments[e, 1:2, :]
    edge = -decay / (1.0 - whole * whole)
    left_state = edge * (right_total - whole * left_total)
    right_state = edge * (left_total - whole * right_total)
    left_own, right_own = left_state, right_state
    for d in range(groups):
        left_own = jnp.where(d == position, left_state, left_own)
        left_state = block * left_state + all_moments[d, 0:1, :]
        e = groups - 1 - d
        right_own = jnp.where(e == position, right_state, right_own)
        right_state = block * right_state + all_moments[e, 1:2, :]
    after_states = []
    for s in range(SEGMENTS):
        left_states[s : s + 1, :] = left_own
        left_own = stride * left_own + left_parts[s : s + 1, :]
        after_states.append(left_own)
    for s in reversed(range(SEGMENTS)):
        right_states[s : s + 1, :] = (right_own + decay * after_states[s]) / root
        right_own = stride * right_own + right_parts[s : s + 1, :]
    for t in range(length // TILE):
        columns = slice(t * TILE, (t + 1) * TILE)
        ratio = jnp.broadcast_to(decay[:, columns], (SEGMENTS, TILE))
        state = left_states[:, columns]
        sums = []
        for g in range(steps):
            state = ratio * state + spectrum[g * SEGMENTS : (g + 1) * SEGMENTS, columns]
            sums.append(state)
        state = right_states[:, columns]
        first = rows * (t * TILE // half)
        inner = slice(t * TILE % half, t * TILE % half + TILE)
        for g in reversed(range(0, steps, 2)):
            later = ratio * (state + sums[g + 1])
            state = ratio * (later + sums[g])
            place = pl.ds(first + g * SEGMENTS, 2 * SEGMENTS)
            high[place, inner], low[place, inner] = split(jnp.concatenate([state, later], axis=0))
    signs = parity((SEGMENTS, LANES))
    blocks = length // LANES
    copies = []
    for t in range(half // TILE):
        table_tile(tables, table_high, table_low, pl.ds(t * TILE, TILE))
        values = product(high, low, table_high, table_low, pl.ds(t * TILE, TILE))
        for c in range(TILE // LANES):
            near = t * TILE // LANES + c
            far = blocks - 1 - near
            columns = slice(c * LANES, (c + 1) * LANES)
            for g in range(steps):
                place = pl.ds(g, SEGMENTS, stride=steps)
                odd = values[g * SEGMENTS : (g + 1) * SEGMENTS, columns]
                even = values[rows + g * SEGMENTS : rows + (g + 1) * SEGMENTS, columns] * signs
                stage[near, place, :] = even + odd
                stage[far, place, :] = mirrored(even - odd)
            for block_index in (near, far):
                target = solved.at[:, pl.ds(block_index * LANES, LANES)]
                copy = pltpu.make_async_copy(stage.at[block_index], target, stored.at[block_index])
                copy.start()
                copies.append(copy)
    for copy in copies:
        copy.wait()


def on_device(source, screening):
    groups = lax.axis_size(GRID_AXES)
    fields, rows, length = source.shape
    half = length // 2
    tables = [jnp.asarray(table) for table in angle_tables(length)]
    cosines = jnp.asarray(double_cosines(length))
    vmem = pl.BlockSpec(memory_space=pltpu.VMEM)
    smem = pl.BlockSpec(memory_space=pltpu.SMEM)
    f32 = lambda *shape: jax.ShapeDtypeStruct(shape, jnp.float32)
    scratch = [
        pltpu.VMEM((2 * rows, half), jnp.bfloat16),
        pltpu.VMEM((2 * rows, half), jnp.bfloat16),
        pltpu.VMEM((half, half), jnp.bfloat16),
        pltpu.VMEM((half, half), jnp.bfloat16),
    ]
    staging = [
        pltpu.VMEM((length // LANES, rows, LANES), jnp.float32),
        pltpu.SemaphoreType.DMA((length // LANES,)),
    ]
    hbm = pl.BlockSpec(memory_space=pl.ANY)
    exchange = [
        pltpu.VMEM((2, length), jnp.float32),
        pltpu.VMEM((groups, 2, length), jnp.float32),
        pltpu.SemaphoreType.DMA((groups,)),
        pltpu.SemaphoreType.DMA((groups,)),
    ]
    parts = (SEGMENTS, length)
    params = pltpu.CompilerParams(vmem_limit_bytes=40 * 2**20)

    def one_field(grid, constant):
        spectrum, left_parts, right_parts, all_moments = pl.pallas_call(
            functools.partial(forward_kernel, groups),
            out_shape=[f32(rows, length), f32(*parts), f32(*parts), f32(groups, 2, length)],
            in_specs=[hbm, smem] + [vmem] * 5,
            out_specs=[vmem] * 4,
            scratch_shapes=scratch + staging + exchange,
            compiler_params=pltpu.CompilerParams(
                vmem_limit_bytes=40 * 2**20, collective_id=0, has_side_effects=True
            ),
            name="forward",
        )(grid, constant, cosines, *tables)
        return pl.pallas_call(
            functools.partial(backward_kernel, groups),
            out_shape=f32(rows, length),
            in_specs=[vmem] * 4 + [smem] + [vmem] * 5,
            out_specs=hbm,
            scratch_shapes=scratch + [pltpu.VMEM(parts, jnp.float32)] * 2 + staging,
            compiler_params=params,
            name="backward",
        )(spectrum, left_parts, right_parts, all_moments, constant, cosines, *tables)

    return jnp.stack([one_field(source[f], screening[f : f + 1]) for f in range(fields)])


def solution(mesh):
    return jax.shard_map(
        on_device,
        mesh=mesh,
        in_specs=(P("af", GRID_AXES, None), P("af")),
        out_specs=P("af", GRID_AXES, None),
        check_vma=False,
    )
```

profile of v0, /device:TPU:0, one launch (start us, length us, event | category | flops | bytes accessed | tf_op | source)
XLA Modules:
  0.0 24.7 jit_solution(3068051243039051089)
XLA Ops:
  0.7 0.0 copy-start
  0.7 1.6 %copy-done = f32[1,256,2048]{2,1,0:T(8,128)S(1)} copy-done((f32[1,256,2048]{2,1,0:T(8,128)S(1)}, f32[1,256,2048]{2,1,0:T(8,128)}, u32[]{:S(2)}) %copy-start) | copy-done | bytes 2097176
  2.2 0.0 copy-start.1
  2.2 0.9 %copy-done.1 = f32[32,1024]{1,0:T(8,128)S(1)} copy-done((f32[32,1024]{1,0:T(8,128)S(1)}, f32[32,1024]{1,0:T(8,128)}, u32[]{:S(2)}) %copy-start.1) | copy-done | bytes 131096
  3.1 0.0 copy-start.2
  3.2 0.9 %copy-done.2 = f32[32,1024]{1,0:T(8,128)S(1)} copy-done((f32[32,1024]{1,0:T(8,128)S(1)}, f32[32,1024]{1,0:T(8,128)}, u32[]{:S(2)}) %copy-start.2) | copy-done | bytes 131096
  4.1 0.0 copy-start.3
  4.1 0.9 %copy-done.3 = f32[32,1024]{1,0:T(8,128)S(1)} copy-done((f32[32,1024]{1,0:T(8,128)S(1)}, f32[32,1024]{1,0:T(8,128)}, u32[]{:S(2)}) %copy-start.3) | copy-done | bytes 131096
  5.0 0.0 copy-start.4
  5.0 0.9 %copy-done.4 = f32[32,1024]{1,0:T(8,128)S(1)} copy-done((f32[32,1024]{1,0:T(8,128)S(1)}, f32[32,1024]{1,0:T(8,128)}, u32[]{:S(2)}) %copy-start.4) | copy-done | bytes 131096
  5.9 0.0 copy-start.5
  5.9 0.7 %copy-done.5 = f32[1,2048]{1,0:T(1,128)S(1)} copy-done((f32[1,2048]{1,0:T(1,128)S(1)}, f32[1,2048]{1,0:T(1,128)}, u32[]{:S(2)}) %copy-start.5) | copy-done | bytes 8216
  6.6 11.4 %forward.1 = (f32[256,2048]{1,0:T(8,128)S(1)}, f32[8,2048]{1,0:T(8,128)S(1)}, f32[8,2048]{1,0:T(8,128)S(1)}, f32[8,2,2048]{2,1,0:T(2,128)S(1)}) custom-call(f32[256,2048]{1,0:T(8,128)S(1)} %bitcast.2, f32[1]{0:T(128)S(6)} %copy.8.screening, f32[1,2048]{1,0:T(1,128)S(1)} %copy-done.5, f32[32,1024]{1,0:T(8,128)S(1)} %copy-done.4, f32[32,1024]{1,0:T(8,128)S(1)} %copy-done.3, ...), custom_call_target="tpu_custom_call" | custom-call | tf_op jit(solution)/shard_map/forward/pallas_call | solution.py:305
  18.0 6.6 %backward.1 = f32[256,2048]{1,0:T(8,128)} custom-call(f32[256,2048]{1,0:T(8,128)S(1)} %get-tuple-element.9.spectrum, f32[8,2048]{1,0:T(8,128)S(1)} %get-tuple-element.10.left_parts, f32[8,2048]{1,0:T(8,128)S(1)} %get-tuple-element.11.right_parts, f32[8,2,2048]{2,1,0:T(2,128)S(1)} %get-tuple-element.12.all_moments, f32[1]{0:T(128)S(6)} %copy.8.screening, ...), custom_call_target="tpu_custom_call" | custom-call | tf_op jit(solution)/shard_map/backward/pallas_call | solution.py:316
Async XLA Ops:
  0.7 1.6 %copy-start = (f32[1,256,2048]{2,1,0:T(8,128)S(1)}, f32[1,256,2048]{2,1,0:T(8,128)}, u32[]{:S(2)}) copy-start(f32[1,256,2048]{2,1,0:T(8,128)} %param.7) | copy-start | bytes 6291460
  2.2 0.9 %copy-start.1 = (f32[32,1024]{1,0:T(8,128)S(1)}, f32[32,1024]{1,0:T(8,128)}, u32[]{:S(2)}) copy-start(f32[32,1024]{1,0:T(8,128)} %constant.13.clone.fine_cos) | copy-start | bytes 393220
  3.1 0.9 %copy-start.2 = (f32[32,1024]{1,0:T(8,128)S(1)}, f32[32,1024]{1,0:T(8,128)}, u32[]{:S(2)}) copy-start(f32[32,1024]{1,0:T(8,128)} %constant.12.clone.fine_sin) | copy-start | bytes 393220
  4.1 0.9 %copy-start.3 = (f32[32,1024]{1,0:T(8,128)S(1)}, f32[32,1024]{1,0:T(8,128)}, u32[]{:S(2)}) copy-start(f32[32,1024]{1,0:T(8,128)} %constant.11.clone.coarse_cos) | copy-start | bytes 393220
  5.0 0.9 %copy-start.4 = (f32[32,1024]{1,0:T(8,128)S(1)}, f32[32,1024]{1,0:T(8,128)}, u32[]{:S(2)}) copy-start(f32[32,1024]{1,0:T(8,128)} %constant.10.clone.coarse_sin) | copy-start | bytes 393220
  5.9 0.7 %copy-start.5 = (f32[1,2048]{1,0:T(1,128)S(1)}, f32[1,2048]{1,0:T(1,128)}, u32[]{:S(2)}) copy-start(f32[1,2048]{1,0:T(1,128)} %constant.14.clone.cosines) | copy-start | bytes 24580
where the time goes:
time: 24.9 us; the launch traced here: 24.7 us
  Pallas kernels  18.1 us (73%)
  local copies, waits for them, and re-layouts  5.9 us (24%)
  between operations  0.67 us (3%)
    pallas_call x1, Pallas kernels, one_field(): pl.pallas_call(functools.partial(forward_kernel, groups), out_shape=[f32(...  11.4 us
    pallas_call x1, Pallas kernels, one_field(): pl.pallas_call(functools.partial(backward_kernel, groups), out_shape=f32(...  6.65 us
    unnamed x12, local copies, waits for them, and re-layouts  5.9 us

commit v1 on v0

v1 whole, which is shorter than its diff:
```python
import functools
import math

import jax
import jax.numpy as jnp
import numpy as np
from jax import lax
from jax.experimental import pallas as pl
from jax.experimental.pallas import tpu as pltpu
from jax.sharding import PartitionSpec as P

LANES = 128
SEGMENTS = 8
TILE = 256
STEP = 32
GRID_AXES = ("gx", "gy")
MESH = pl.DeviceIdType.MESH


def mode_numbers(length):
    half = length // 2
    numbers = np.arange(half, dtype=np.int64) + 1
    return np.concatenate([2 * numbers, length + 1 - 2 * numbers])


def double_cosines(length):
    angles = mode_numbers(length).astype(np.float32) * np.float32(math.pi / (length + 1))
    return np.float32(2.0) * np.cos(angles.astype(np.float64)).astype(np.float32)


def constant_rows(length):
    half = length // 2
    columns = np.arange(half, dtype=np.int64)[None, :] + 1
    coarse = np.arange(half // STEP, dtype=np.int64)[:, None] * STEP
    fine = np.arange(STEP, dtype=np.int64)[:, None] + 1
    scale = math.sqrt(2.0 / (length + 1))
    angle = lambda rows: 2.0 * math.pi * (rows * columns % (length + 1)) / (length + 1)
    tables = (
        scale * np.sin(angle(coarse)),
        scale * np.cos(angle(coarse)),
        np.sin(angle(fine)),
        np.cos(angle(fine)),
        double_cosines(length).reshape(2, half),
        np.zeros((SEGMENTS - 2, half)),
    )
    return np.concatenate(tables).astype(np.float32)


def power(base, exponent):
    result = None
    while exponent:
        if exponent & 1:
            result = base if result is None else result * base
        exponent >>= 1
        if exponent:
            base = base * base
    return result


def decay_of(screening, cosines):
    factor = (4.0 + screening) - cosines
    excess = factor - 2.0
    root = jnp.sqrt(excess * (excess + 4.0))
    return 2.0 / (factor + root), root


def split(values):
    high = values.astype(jnp.bfloat16)
    return high, (values - high.astype(jnp.float32)).astype(jnp.bfloat16)


def mirrored(values):
    lanes = lax.broadcasted_iota(jnp.int32, values.shape, 1)
    return jnp.take_along_axis(values, LANES - 1 - lanes, axis=1)


def parity(shape):
    lanes = lax.broadcasted_iota(jnp.int32, shape, 1)
    return jnp.where(lanes % 2 == 0, 1.0, -1.0)


def tile_columns(t):
    return slice(t * TILE, (t + 1) * TILE)


def product(high, low, table_high, table_low):
    dot = functools.partial(jnp.dot, preferred_element_type=jnp.float32)
    return dot(high, table_high) + dot(low, table_high) + dot(high, table_low)


def peer(index):
    across = lax.axis_size("gy")
    return {"gx": index // across, "gy": index % across}


def boundary_states(groups, rows, moments_of, decay, root, left_parts, right_parts, left_states, right_states):
    position = lax.axis_index(GRID_AXES)
    stride = power(decay, rows // SEGMENTS)
    block = power(decay, rows)
    whole = power(decay, rows * groups + 1)
    moments = [moments_of((position + groups - d) % groups) for d in range(groups)]
    left_total = right_total = jnp.zeros_like(decay)
    for d in range(groups):
        left_total = block * left_total + moments[d][0:1, :]
        right_total = block * right_total + moments[groups - 1 - d][1:2, :]
    edge = -decay / (1.0 - whole * whole)
    left_state = edge * (right_total - whole * left_total)
    right_state = edge * (left_total - whole * right_total)
    left_own, right_own = left_state, right_state
    for d in range(groups):
        left_own = jnp.where(d == position, left_state, left_own)
        left_state = block * left_state + moments[d][0:1, :]
        e = groups - 1 - d
        right_own = jnp.where(e == position, right_state, right_own)
        right_state = block * right_state + moments[e][1:2, :]
    after_states = []
    for s in range(SEGMENTS):
        left_states[s : s + 1, :] = left_own
        left_own = stride * left_own + left_parts[s : s + 1, :]
        after_states.append(left_own)
    for s in reversed(range(SEGMENTS)):
        right_states[s : s + 1, :] = (right_own + decay * after_states[s]) / root
        right_own = stride * right_own + right_parts[s : s + 1, :]


def solve_lines(spectrum, decay, left_states, right_states, high, low):
    rows = spectrum.shape[0]
    steps = rows // SEGMENTS
    for h in range(2):
        columns = tile_columns(h)
        ratio = jnp.broadcast_to(decay[:, columns], (SEGMENTS, TILE))
        state = left_states[:, columns]
        sums = []
        for g in range(steps):
            state = ratio * state + spectrum[g * SEGMENTS : (g + 1) * SEGMENTS, columns]
            sums.append(state)
        state = right_states[:, columns]
        for g in reversed(range(0, steps, 2)):
            later = ratio * (state + sums[g + 1])
            state = ratio * (later + sums[g])
            place = pl.ds(h * rows + g * SEGMENTS, 2 * SEGMENTS)
            high[place, :], low[place, :] = split(jnp.concatenate([state, later], axis=0))


def line_sums(spectrum, decay, left_parts, right_parts):
    rows = spectrum.shape[0]
    steps = rows // SEGMENTS
    for h in range(2):
        columns = tile_columns(h)
        ratio = jnp.broadcast_to(decay[:, columns], (SEGMENTS, TILE))
        left = right = jnp.zeros((SEGMENTS, TILE), jnp.float32)
        for g in range(steps):
            mirror = steps - 1 - g
            left = ratio * left + spectrum[g * SEGMENTS : (g + 1) * SEGMENTS, columns]
            right = ratio * right + spectrum[mirror * SEGMENTS : (mirror + 1) * SEGMENTS, columns]
        left_parts[:, columns] = left
        right_parts[:, columns] = right


def forward_kernel(
    groups, pitch, source, screening, constants,
    table_high, table_low, partial, next_high, next_low,
    last_spectrum, last_left, last_right, last_moments, last_decay,
    rows_of, rows_sems, stage, arrived, high, low, back_high, back_low,
    spectrum, left_parts, right_parts, left_states, right_states,
    landed, send_sems, recv_sems,
):
    _, steps, length = source.shape
    rows = SEGMENTS * steps
    half = length // 2
    blocks = length // LANES
    tiles = half // TILE
    steps = rows // SEGMENTS
    last = tiles - 1
    position = lax.axis_index(GRID_AXES)

    rows_copies = [
        pltpu.make_async_copy(
            constants.at[:, pl.ds(t * TILE, TILE)], rows_of.at[:, pl.ds(t * TILE, TILE)], rows_sems.at[t]
        )
        for t in range(tiles)
    ]
    copies = [
        pltpu.make_async_copy(
            source.at[:, :, pl.ds(c * LANES, LANES)],
            stage.at[c].reshape(SEGMENTS, pitch, LANES).at[:, pl.ds(0, steps), :],
            arrived.at[c],
        )
        for c in range(blocks)
    ]
    rows_copies[0].start()
    for c in range(blocks // 2):
        copies[c].start()
        copies[blocks - 1 - c].start()
    for copy in rows_copies[1:]:
        copy.start()
    barrier = pltpu.get_barrier_semaphore()
    for d in range(1, groups):
        pl.semaphore_signal(barrier, inc=1, device_id=peer((position + d) % groups), device_id_type=MESH)

    def make_table(t):
        columns = tile_columns(t)
        fine_sin = rows_of[2 * coarse_rows : 2 * coarse_rows + STEP, columns]
        fine_cos = rows_of[2 * coarse_rows + STEP : 2 * coarse_rows + 2 * STEP, columns]
        for a in range(coarse_rows):
            values = rows_of[a : a + 1, columns] * fine_cos + rows_of[coarse_rows + a : coarse_rows + a + 1, columns] * fine_sin
            place = slice(a * STEP, (a + 1) * STEP)
            table_high[place, columns], table_low[place, columns] = split(values)

    coarse_rows = half // STEP
    cosine_row = 2 * coarse_rows + 2 * STEP

    def decay_tile(t):
        columns = tile_columns(t)
        cosines = [rows_of[cosine_row + h : cosine_row + h + 1, columns] for h in range(2)]
        return decay_of(screening[0], jnp.concatenate(cosines, axis=1))

    rows_copies[0].wait()
    make_table(0)
    signs = parity((2 * SEGMENTS, LANES))
    for c in range(blocks // 2):
        copies[c].wait()
        copies[blocks - 1 - c].wait()
        columns = pl.ds(c * LANES, LANES)
        for g in range(0, steps, 2):
            place = pl.ds(g * SEGMENTS, 2 * SEGMENTS)
            place_sum = pl.ds(rows + g * SEGMENTS, 2 * SEGMENTS)

            def load(column):
                pair = [stage[column, pl.ds(g + e, SEGMENTS, stride=pitch), :] for e in range(2)]
                return jnp.concatenate(pair, axis=0)

            near = load(c)
            far = mirrored(load(blocks - 1 - c))
            high[place, columns], low[place, columns] = split(near - far)
            high[place_sum, columns], low[place_sum, columns] = split((near + far) * signs)
    for copy in rows_copies[1:]:
        copy.wait()

    def lines_of(t):
        return last_spectrum if t == last else spectrum.at[t]

    def sums_of(t):
        return (last_left, last_right) if t == last else (left_parts.at[t], right_parts.at[t])

    sends = []
    for t in range(tiles):
        columns = tile_columns(t)
        values = product(high[...], low[...], table_high[:, columns], table_low[:, columns])
        if t + 1 < tiles:
            make_table(t + 1)
        lines_of(t)[:, :TILE] = values[:rows]
        lines_of(t)[:, TILE:] = values[rows:]
        decay, root = decay_tile(t)
        left_sums, right_sums = sums_of(t)
        line_sums(lines_of(t), decay, left_sums, right_sums)
        stride = power(decay, steps)
        left = right = jnp.zeros_like(decay)
        for s in range(SEGMENTS):
            left = stride * left + left_sums[s : s + 1, :]
            right = stride * right + right_sums[SEGMENTS - 1 - s : SEGMENTS - s, :]
        landed[t, 0, 0:1, :] = left
        landed[t, 0, 1:2, :] = right
        if t == 0:
            pl.semaphore_wait(barrier, groups - 1)
        for d in range(1, groups):
            send = pltpu.make_async_remote_copy(
                src_ref=landed.at[t, 0],
                dst_ref=landed.at[t, d],
                send_sem=send_sems.at[t, d],
                recv_sem=recv_sems.at[t, d],
                device_id=peer((position + d) % groups),
                device_id_type=MESH,
            )
            send.start()
            sends.append(send)
    last_decay[0:1, :], last_decay[1:2, :] = decay, root

    def receive(t):
        for send in sends[t * (groups - 1) : (t + 1) * (groups - 1)]:
            send.wait_recv()

    def multiply(t):
        inner = slice(t * TILE, (t + 1) * TILE)
        for n in range(tiles):
            columns = tile_columns(n)
            values = product(back_high[t], back_low[t], table_high[inner, columns], table_low[inner, columns])
            partial[:, columns] = values if t == 0 else partial[:, columns] + values

    if last < 2:
        partial[...] = jnp.zeros_like(partial)
    for t in range(last):
        receive(t)
        if t:
            multiply(t - 1)
        decay, root = decay_tile(t)
        boundary_states(
            groups, rows, lambda index, t=t: landed[t, index], decay, root,
            left_parts.at[t], right_parts.at[t], left_states.at[t], right_states.at[t],
        )
        target = (next_high, next_low) if t == last - 1 else (back_high.at[t], back_low.at[t])
        solve_lines(spectrum.at[t], decay, left_states.at[t], right_states.at[t], *target)
    receive(last)
    for d in range(groups):
        last_moments[d] = landed[last, d]
    for send in sends:
        send.wait_send()


def backward_kernel(
    groups, pitch, table_high, table_low, partial, next_high, next_low,
    last_spectrum, last_left, last_right, last_moments, last_decay,
    solved, acc, last_high, last_low, left_states, right_states, stage, stored,
):
    _, steps, length = solved.shape
    rows = SEGMENTS * steps
    half = length // 2
    blocks = length // LANES
    tiles = half // TILE
    steps = rows // SEGMENTS
    before = slice((tiles - 2) * TILE, (tiles - 1) * TILE)
    inner = slice((tiles - 1) * TILE, tiles * TILE)
    for n in range(tiles):
        columns = tile_columns(n)
        acc[:, columns] = partial[:, columns] + product(
            next_high[...], next_low[...], table_high[before, columns], table_low[before, columns]
        )
    decay, root = last_decay[0:1, :], last_decay[1:2, :]
    boundary_states(
        groups, rows, lambda index: last_moments[index], decay, root, last_left, last_right, left_states, right_states
    )
    solve_lines(last_spectrum, decay, left_states, right_states, last_high, last_low)
    signs = parity((SEGMENTS, LANES))
    copies = []
    for n in range(tiles):
        columns = tile_columns(n)
        values = acc[:, columns] + product(
            last_high[...], last_low[...], table_high[inner, columns], table_low[inner, columns]
        )
        for c in range(TILE // LANES):
            near = n * TILE // LANES + c
            far = blocks - 1 - near
            lanes = slice(c * LANES, (c + 1) * LANES)
            for g in range(steps):
                place = pl.ds(g, SEGMENTS, stride=pitch)
                odd = values[g * SEGMENTS : (g + 1) * SEGMENTS, lanes]
                even = values[rows + g * SEGMENTS : rows + (g + 1) * SEGMENTS, lanes] * signs
                stage[near, place, :] = even + odd
                stage[far, place, :] = mirrored(even - odd)
            for index in (near, far):
                copy = pltpu.make_async_copy(
                    stage.at[index].reshape(SEGMENTS, pitch, LANES).at[:, pl.ds(0, steps), :],
                    solved.at[:, :, pl.ds(index * LANES, LANES)],
                    stored.at[index],
                )
                copy.start()
                copies.append(copy)
    for copy in copies:
        copy.wait()


def on_device(source, screening):
    groups = lax.axis_size(GRID_AXES)
    fields, rows, length = source.shape
    half = length // 2
    tiles = half // TILE
    width = 2 * TILE
    steps = rows // SEGMENTS
    pitch = steps + 8 if steps % 16 == 0 else steps
    blocks = length // LANES
    constants = jnp.asarray(constant_rows(length))
    vmem = pl.BlockSpec(memory_space=pltpu.VMEM)
    smem = pl.BlockSpec(memory_space=pltpu.SMEM)
    hbm = pl.BlockSpec(memory_space=pl.ANY)
    f32 = lambda *shape: jax.ShapeDtypeStruct(shape, jnp.float32)
    bf16 = lambda *shape: jax.ShapeDtypeStruct(shape, jnp.bfloat16)
    stay = lambda array: pltpu.with_memory_space_constraint(array, pltpu.HBM)
    floats = lambda *shape: pltpu.VMEM(shape, jnp.float32)
    halves = lambda *shape: pltpu.VMEM(shape, jnp.bfloat16)
    staging = [floats(blocks, SEGMENTS * pitch, LANES), pltpu.SemaphoreType.DMA((blocks,))]

    def one_field(grid, constant):
        parts = pl.pallas_call(
            functools.partial(forward_kernel, groups, pitch),
            out_shape=[
                bf16(half, half), bf16(half, half), f32(2 * rows, half),
                bf16(2 * rows, TILE), bf16(2 * rows, TILE),
                f32(rows, width), f32(SEGMENTS, width), f32(SEGMENTS, width),
                f32(groups, 2, width), f32(2, width),
            ],
            in_specs=[hbm, smem, hbm],
            out_specs=[vmem] * 10,
            scratch_shapes=[floats(*constants.shape), pltpu.SemaphoreType.DMA((tiles,))]
            + staging
            + [halves(2 * rows, half)] * 2
            + [halves(tiles - 2, 2 * rows, TILE)] * 2
            + [floats(tiles - 1, rows, width)]
            + [floats(tiles - 1, SEGMENTS, width)] * 4
            + [floats(tiles, groups, 2, width)]
            + [pltpu.SemaphoreType.DMA((tiles, groups))] * 2,
            compiler_params=pltpu.CompilerParams(
                vmem_limit_bytes=40 * 2**20, collective_id=0, has_side_effects=True
            ),
            name="forward",
        )(stay(grid.reshape(SEGMENTS, steps, length)), constant, stay(constants))
        solved = pl.pallas_call(
            functools.partial(backward_kernel, groups, pitch),
            out_shape=f32(SEGMENTS, steps, length),
            in_specs=[vmem] * 10,
            out_specs=hbm,
            scratch_shapes=[floats(2 * rows, half)]
            + [halves(2 * rows, TILE)] * 2
            + [floats(SEGMENTS, width)] * 2
            + staging,
            compiler_params=pltpu.CompilerParams(vmem_limit_bytes=40 * 2**20),
            name="backward",
        )(*parts)
        return solved.reshape(rows, length)

    return jnp.stack([one_field(source[f], screening[f : f + 1]) for f in range(fields)])


def solution(mesh):
    return jax.shard_map(
        on_device,
        mesh=mesh,
        in_specs=(P("af", GRID_AXES, None), P("af")),
        out_specs=P("af", GRID_AXES, None),
        check_vma=False,
    )
```

time: 24.9 us -> 22.2 us (0.89)
  local copies, waits for them, and re-layouts: 5.9 us -> 0 us
  Pallas kernels: 18.1 us -> 21.4 us
    unnamed x12 -> x0, local copies, waits for them, and re-layouts: 5.9 us -> none
    pallas_call x2, Pallas kernels: 18.1 us -> 21.4 us  [the longest x1 16.9 us: one_field(): pl.pallas_call(functools.partial(forward_kernel, groups, pitch), out_shap...]
where the time goes in v1:
time: 22.2 us; the launch traced here: 22.1 us
  Pallas kernels  21.4 us (96%)
  between operations  0.66 us (3%)
    pallas_call x1, Pallas kernels, one_field(): pl.pallas_call(functools.partial(forward_kernel, groups, pitch), out_shap...  16.9 us
    pallas_call x1, Pallas kernels, one_field(): pl.pallas_call(functools.partial(backward_kernel, groups, pitch), out_sha...  4.48 us

profile of v1, /device:TPU:0, one launch (start us, length us, event | category | flops | bytes accessed | tf_op | source)
XLA Modules:
  0.0 22.1 jit_solution(17570473617773073476)
XLA Ops:
  0.7 16.9 %forward.1 = (bf16[1024,1024]{1,0:T(8,128)(2,1)S(1)}, bf16[1024,1024]{1,0:T(8,128)(2,1)S(1)}, f32[512,1024]{1,0:T(8,128)S(1)}, bf16[512,256]{1,0:T(8,128)(2,1)S(...) custom-call(f32[8,32,2048]{2,1,0:T(8,128)} %bitcast.2, ...), custom_call_target="tpu_custom_call" | custom-call | tf_op jit(solution)/shard_map/forward/pallas_call | solution.py:383
  17.6 4.5 %backward.1 = f32[8,32,2048]{2,1,0:T(8,128)} custom-call(bf16[1024,1024]{1,0:T(8,128)(2,1)S(1)} %get-tuple-element.15.table_high, bf16[1024,1024]{1,0:T(8,128)(2,1)S(1)} %get-tuple-element.16.table_low, f32[512,1024]{1,0:T(8,128)S(1)} %get-tuple-element.17.partial, bf16[512,256]{1,0:T(8,128)(2,1)S(1)} %get-tuple-element.18.next_high, ...), custom_call_target="tpu_custom_call" | custom-call | tf_op jit(solution)/shard_map/backward/pallas_call | solution.py:406

commit v2 on v1

v2 whole, which is shorter than its diff:
```python
import functools
import math

import jax
import jax.numpy as jnp
import numpy as np
from jax import lax
from jax.experimental import pallas as pl
from jax.experimental.pallas import tpu as pltpu
from jax.sharding import PartitionSpec as P

LANES = 128
SEGMENTS = 8
TILE = 256
STEP = 32
COEFFICIENTS = 6
GRID_AXES = ("gx", "gy")
MESH = pl.DeviceIdType.MESH


def mode_numbers(length):
    half = length // 2
    numbers = np.arange(half, dtype=np.int64) + 1
    return np.concatenate([2 * numbers, length + 1 - 2 * numbers])


def double_cosines(length):
    angles = mode_numbers(length).astype(np.float32) * np.float32(math.pi / (length + 1))
    return np.float32(2.0) * np.cos(angles.astype(np.float64)).astype(np.float32)


def constant_rows(length):
    half = length // 2
    columns = np.arange(half, dtype=np.int64)[None, :] + 1
    coarse = np.arange(half // STEP, dtype=np.int64)[:, None] * STEP
    fine = np.arange(STEP, dtype=np.int64)[:, None] + 1
    scale = math.sqrt(2.0 / (length + 1))
    angle = lambda rows: 2.0 * math.pi * (rows * columns % (length + 1)) / (length + 1)
    tables = (
        scale * np.sin(angle(coarse)),
        scale * np.cos(angle(coarse)),
        np.sin(angle(fine)),
        np.cos(angle(fine)),
    )
    return np.concatenate(tables).astype(np.float32)


def cosine_rows(length):
    tiles = length // (2 * TILE)
    rows = double_cosines(length).reshape(2, tiles, TILE).transpose(1, 0, 2).reshape(tiles, 2 * TILE)
    return np.concatenate([rows, np.repeat(rows[-1:], -tiles % SEGMENTS, axis=0)])


def power(base, exponent):
    result = None
    while exponent:
        if exponent & 1:
            result = base if result is None else result * base
        exponent >>= 1
        if exponent:
            base = base * base
    return result


def decay_of(screening, cosines):
    factor = (4.0 + screening) - cosines
    excess = factor - 2.0
    root = jnp.sqrt(excess * (excess + 4.0))
    return 2.0 / (factor + root), root


def split(values):
    high = values.astype(jnp.bfloat16)
    return high, (values - high.astype(jnp.float32)).astype(jnp.bfloat16)


def mirrored(values):
    lanes = lax.broadcasted_iota(jnp.int32, values.shape, 1)
    return jnp.take_along_axis(values, LANES - 1 - lanes, axis=1)


def parity(shape):
    lanes = lax.broadcasted_iota(jnp.int32, shape, 1)
    return jnp.where(lanes % 2 == 0, 1.0, -1.0)


def tile_columns(t):
    return slice(t * TILE, (t + 1) * TILE)


def product(high, low, table_high, table_low):
    dot = functools.partial(jnp.dot, preferred_element_type=jnp.float32)
    return dot(high, table_high) + dot(low, table_high) + dot(high, table_low)


def peer(index):
    across = lax.axis_size("gy")
    return {"gx": index // across, "gy": index % across}


def store_coefficients(groups, rows, screening, cosines, coefficients):
    decay, root = decay_of(screening, cosines)
    whole = power(decay, rows * groups + 1)
    values = (
        decay,
        power(decay, rows // SEGMENTS),
        power(decay, rows),
        whole,
        -decay / (1.0 - whole * whole),
        1.0 / root,
    )
    for index, value in enumerate(values):
        coefficients[index] = value


def boundary_states(groups, moments_of, coefficients, left_parts, right_parts, left_states, right_states):
    decay, stride, block, whole, edge, scale = coefficients
    position = lax.axis_index(GRID_AXES)
    moments = [moments_of((position + groups - d) % groups) for d in range(groups)]
    left_total = right_total = jnp.zeros_like(decay)
    for d in range(groups):
        left_total = block * left_total + moments[d][0:1, :]
        right_total = block * right_total + moments[groups - 1 - d][1:2, :]
    left_state = edge * (right_total - whole * left_total)
    right_state = edge * (left_total - whole * right_total)
    left_own, right_own = left_state, right_state
    for d in range(groups):
        left_own = jnp.where(d == position, left_state, left_own)
        left_state = block * left_state + moments[d][0:1, :]
        e = groups - 1 - d
        right_own = jnp.where(e == position, right_state, right_own)
        right_state = block * right_state + moments[e][1:2, :]
    after_states = []
    for s in range(SEGMENTS):
        left_states[s : s + 1, :] = left_own
        left_own = stride * left_own + left_parts[s : s + 1, :]
        after_states.append(left_own)
    for s in reversed(range(SEGMENTS)):
        right_states[s : s + 1, :] = (right_own + decay * after_states[s]) * scale
        right_own = stride * right_own + right_parts[s : s + 1, :]


def solve_lines(spectrum, decay, left_states, right_states, high, low):
    rows = spectrum.shape[0]
    steps = rows // SEGMENTS
    for h in range(2):
        columns = tile_columns(h)
        ratio = jnp.broadcast_to(decay[:, columns], (SEGMENTS, TILE))
        state = left_states[:, columns]
        sums = []
        for g in range(steps):
            state = ratio * state + spectrum[g * SEGMENTS : (g + 1) * SEGMENTS, columns]
            sums.append(state)
        state = right_states[:, columns]
        for g in reversed(range(0, steps, 2)):
            later = ratio * (state + sums[g + 1])
            state = ratio * (later + sums[g])
            place = pl.ds(h * rows + g * SEGMENTS, 2 * SEGMENTS)
            high[place, :], low[place, :] = split(jnp.concatenate([state, later], axis=0))


def line_sums(spectrum, decay, stride, left_parts, right_parts, moments):
    rows = spectrum.shape[0]
    steps = rows // SEGMENTS
    for h in range(2):
        columns = tile_columns(h)
        ratio = jnp.broadcast_to(decay[:, columns], (SEGMENTS, TILE))
        left = right = jnp.zeros((SEGMENTS, TILE), jnp.float32)
        for g in range(steps):
            mirror = steps - 1 - g
            left = ratio * left + spectrum[g * SEGMENTS : (g + 1) * SEGMENTS, columns]
            right = ratio * right + spectrum[mirror * SEGMENTS : (mirror + 1) * SEGMENTS, columns]
        left_parts[:, columns] = left
        right_parts[:, columns] = right
    left = right = jnp.zeros_like(decay)
    for s in range(SEGMENTS):
        left = stride * left + left_parts[s : s + 1, :]
        right = stride * right + right_parts[SEGMENTS - 1 - s : SEGMENTS - s, :]
    moments[0:1, :] = left
    moments[1:2, :] = right


def forward_kernel(
    groups, pitch, source, screening, constants, cosines,
    table_high, table_low, partial, next_high, next_low,
    last_spectrum, last_left, last_right, last_moments, coefficients,
    angles, angle_sems, cosines_here, cosines_sem, stage, arrived, high, low, back_high, back_low,
    spectrum, left_parts, right_parts, left_states, right_states,
    landed, send_sems, recv_sems,
):
    _, steps, length = source.shape
    rows = SEGMENTS * steps
    half = length // 2
    blocks = length // LANES
    tiles = half // TILE
    last = tiles - 1
    position = lax.axis_index(GRID_AXES)

    angle_copies = [
        pltpu.make_async_copy(
            constants.at[:, pl.ds(t * TILE, TILE)], angles.at[:, pl.ds(t * TILE, TILE)], angle_sems.at[t]
        )
        for t in range(tiles)
    ]
    cosines_copy = pltpu.make_async_copy(cosines, cosines_here, cosines_sem.at[0])
    copies = [
        pltpu.make_async_copy(
            source.at[:, :, pl.ds(c * LANES, LANES)],
            stage.at[c].reshape(SEGMENTS, pitch, LANES).at[:, pl.ds(0, steps), :],
            arrived.at[c],
        )
        for c in range(blocks)
    ]
    angle_copies[0].start()
    cosines_copy.start()
    for c in range(blocks // 2):
        copies[c].start()
        copies[blocks - 1 - c].start()
    for copy in angle_copies[1:]:
        copy.start()
    barrier = pltpu.get_barrier_semaphore()
    for d in range(1, groups):
        pl.semaphore_signal(barrier, inc=1, device_id=peer((position + d) % groups), device_id_type=MESH)

    coarse_rows = half // STEP

    def make_table(t):
        columns = tile_columns(t)
        fine_sin = angles[2 * coarse_rows : 2 * coarse_rows + STEP, columns]
        fine_cos = angles[2 * coarse_rows + STEP : 2 * coarse_rows + 2 * STEP, columns]
        for a in range(coarse_rows):
            coarse_sin = angles[a : a + 1, columns]
            coarse_cos = angles[coarse_rows + a : coarse_rows + a + 1, columns]
            place = slice(a * STEP, (a + 1) * STEP)
            table_high[place, columns], table_low[place, columns] = split(coarse_sin * fine_cos + coarse_cos * fine_sin)

    def row_of(index, t):
        return coefficients[index, t : t + 1, :]

    angle_copies[0].wait()
    cosines_copy.wait()
    store_coefficients(groups, rows, screening[0], cosines_here[...], coefficients)
    make_table(0)
    signs = parity((2 * SEGMENTS, LANES))
    pairs = blocks // 2
    for begin in range(0, pairs, pairs // 2):
        chosen = range(begin, begin + pairs // 2)
        for c in chosen:
            copies[c].wait()
            copies[blocks - 1 - c].wait()
        for c in chosen:
            columns = pl.ds(c * LANES, LANES)
            for g in range(0, steps, 2):
                place = pl.ds(g * SEGMENTS, 2 * SEGMENTS)
                place_sum = pl.ds(rows + g * SEGMENTS, 2 * SEGMENTS)

                def load(column):
                    pair = [stage[column, pl.ds(g + e, SEGMENTS, stride=pitch), :] for e in range(2)]
                    return jnp.concatenate(pair, axis=0)

                near = load(c)
                far = mirrored(load(blocks - 1 - c))
                high[place, columns], low[place, columns] = split(near - far)
                high[place_sum, columns], low[place_sum, columns] = split((near + far) * signs)
    for copy in angle_copies[1:]:
        copy.wait()
    pl.semaphore_wait(barrier, groups - 1)

    def lines_of(t):
        return last_spectrum if t == last else spectrum.at[t]

    def sums_of(t):
        return (last_left, last_right) if t == last else (left_parts.at[t], right_parts.at[t])

    def transform(t, h):
        columns = tile_columns(t)
        for k in range(2):
            part = slice(k * rows // 2, (k + 1) * rows // 2)
            place = slice(h * rows + k * rows // 2, h * rows + (k + 1) * rows // 2)
            lines_of(t)[part, tile_columns(h)] = product(
                high[place, :], low[place, :], table_high[:, columns], table_low[:, columns]
            )

    sends = []

    def sum_lines(t):
        line_sums(lines_of(t), row_of(0, t), row_of(1, t), *sums_of(t), landed.at[t, 0])

    def send(t):
        for d in range(1, groups):
            copy = pltpu.make_async_remote_copy(
                src_ref=landed.at[t, 0],
                dst_ref=landed.at[t, d],
                send_sem=send_sems.at[t, d],
                recv_sem=recv_sems.at[t, d],
                device_id=peer((position + d) % groups),
                device_id_type=MESH,
            )
            copy.start()
            sends.append(copy)

    for t in range(tiles):
        transform(t, 0)
        if t:
            sum_lines(t - 1)
            send(t - 1)
        transform(t, 1)
        if t < last:
            make_table(t + 1)
    sum_lines(last)
    send(last)

    def receive(t):
        for copy in sends[t * (groups - 1) : (t + 1) * (groups - 1)]:
            copy.wait_recv()

    def multiply(t):
        inner = slice(t * TILE, (t + 1) * TILE)
        for n in range(tiles):
            columns = tile_columns(n)
            for h in range(2):
                place = slice(h * rows, (h + 1) * rows)
                values = product(
                    back_high[t, place, :], back_low[t, place, :], table_high[inner, columns], table_low[inner, columns]
                )
                partial[place, columns] = values if t == 0 else partial[place, columns] + values

    if last < 2:
        partial[...] = jnp.zeros_like(partial)
    for t in range(last):
        receive(t)
        if t:
            multiply(t - 1)
        boundary_states(
            groups, lambda index, t=t: landed[t, index], [row_of(i, t) for i in range(COEFFICIENTS)],
            left_parts.at[t], right_parts.at[t], left_states.at[t], right_states.at[t],
        )
        target = (next_high, next_low) if t == last - 1 else (back_high.at[t], back_low.at[t])
        solve_lines(spectrum.at[t], row_of(0, t), left_states.at[t], right_states.at[t], *target)
    receive(last)
    for d in range(groups):
        last_moments[d] = landed[last, d]
    for copy in sends:
        copy.wait_send()


def backward_kernel(
    groups, pitch, table_high, table_low, partial, next_high, next_low,
    last_spectrum, last_left, last_right, last_moments, coefficients,
    solved, acc, last_high, last_low, left_states, right_states, stage, stored,
):
    _, steps, length = solved.shape
    rows = SEGMENTS * steps
    half = length // 2
    blocks = length // LANES
    tiles = half // TILE
    before = slice((tiles - 2) * TILE, (tiles - 1) * TILE)
    inner = slice((tiles - 1) * TILE, tiles * TILE)

    def multiply(lines_high, lines_low, inner, n, base):
        columns = tile_columns(n)
        values = []
        for h in range(2):
            place = slice(h * rows, (h + 1) * rows)
            values.append(
                base[place, columns]
                + product(lines_high[place, :], lines_low[place, :], table_high[inner, columns], table_low[inner, columns])
            )
        return values

    for n in range(tiles):
        odd, even = multiply(next_high, next_low, before, n, partial)
        acc[:rows, tile_columns(n)] = odd
        acc[rows:, tile_columns(n)] = even
    row_values = [coefficients[i, tiles - 1 : tiles, :] for i in range(COEFFICIENTS)]
    boundary_states(
        groups, lambda index: last_moments[index], row_values, last_left, last_right, left_states, right_states
    )
    solve_lines(last_spectrum, row_values[0], left_states, right_states, last_high, last_low)
    signs = parity((SEGMENTS, LANES))
    copies = []
    later = multiply(last_high, last_low, inner, 0, acc)
    for n in range(tiles):
        odds, evens = later
        if n + 1 < tiles:
            later = multiply(last_high, last_low, inner, n + 1, acc)
        for c in range(TILE // LANES):
            near = n * TILE // LANES + c
            far = blocks - 1 - near
            lanes = slice(c * LANES, (c + 1) * LANES)
            for g in range(steps):
                place = pl.ds(g, SEGMENTS, stride=pitch)
                odd = odds[g * SEGMENTS : (g + 1) * SEGMENTS, lanes]
                even = evens[g * SEGMENTS : (g + 1) * SEGMENTS, lanes] * signs
                stage[near, place, :] = even + odd
                stage[far, place, :] = mirrored(even - odd)
        for c in range(TILE // LANES):
            near = n * TILE // LANES + c
            for index in (near, blocks - 1 - near):
                copy = pltpu.make_async_copy(
                    stage.at[index].reshape(SEGMENTS, pitch, LANES).at[:, pl.ds(0, steps), :],
                    solved.at[:, :, pl.ds(index * LANES, LANES)],
                    stored.at[index],
                )
                copy.start()
                copies.append(copy)
    for copy in copies:
        copy.wait()


def on_device(source, screening):
    groups = lax.axis_size(GRID_AXES)
    fields, rows, length = source.shape
    half = length // 2
    tiles = half // TILE
    width = 2 * TILE
    steps = rows // SEGMENTS
    pitch = steps + 8 if steps % 16 == 0 else steps
    blocks = length // LANES
    constants = jnp.asarray(constant_rows(length))
    cosines = jnp.asarray(cosine_rows(length))
    vmem = pl.BlockSpec(memory_space=pltpu.VMEM)
    hbm = pl.BlockSpec(memory_space=pl.ANY)
    f32 = lambda *shape: jax.ShapeDtypeStruct(shape, jnp.float32)
    bf16 = lambda *shape: jax.ShapeDtypeStruct(shape, jnp.bfloat16)
    stay = lambda array: pltpu.with_memory_space_constraint(array, pltpu.HBM)
    floats = lambda *shape: pltpu.VMEM(shape, jnp.float32)
    halves = lambda *shape: pltpu.VMEM(shape, jnp.bfloat16)
    staging = [floats(blocks, SEGMENTS * pitch, LANES), pltpu.SemaphoreType.DMA((blocks,))]

    def one_field(grid, constant):
        parts = pl.pallas_call(
            functools.partial(forward_kernel, groups, pitch),
            out_shape=[
                bf16(half, half), bf16(half, half), f32(2 * rows, half),
                bf16(2 * rows, TILE), bf16(2 * rows, TILE),
                f32(rows, width), f32(SEGMENTS, width), f32(SEGMENTS, width),
                f32(groups, 2, width), f32(COEFFICIENTS, *cosines.shape),
            ],
            in_specs=[hbm, pl.BlockSpec(memory_space=pltpu.SMEM), hbm, hbm],
            out_specs=[vmem] * 10,
            scratch_shapes=[
                floats(*constants.shape), pltpu.SemaphoreType.DMA((tiles,)),
                floats(*cosines.shape), pltpu.SemaphoreType.DMA((1,)),
            ]
            + staging
            + [halves(2 * rows, half)] * 2
            + [halves(tiles - 2, 2 * rows, TILE)] * 2
            + [floats(tiles - 1, rows, width)]
            + [floats(tiles - 1, SEGMENTS, width)] * 4
            + [floats(tiles, groups, 2, width)]
            + [pltpu.SemaphoreType.DMA((tiles, groups))] * 2,
            compiler_params=pltpu.CompilerParams(
                vmem_limit_bytes=40 * 2**20, collective_id=0, has_side_effects=True
            ),
            name="forward",
        )(stay(grid.reshape(SEGMENTS, steps, length)), constant, stay(constants), stay(cosines))
        solved = pl.pallas_call(
            functools.partial(backward_kernel, groups, pitch),
            out_shape=f32(SEGMENTS, steps, length),
            in_specs=[vmem] * 10,
            out_specs=hbm,
            scratch_shapes=[floats(2 * rows, half)]
            + [halves(2 * rows, TILE)] * 2
            + [floats(SEGMENTS, width)] * 2
            + staging,
            compiler_params=pltpu.CompilerParams(vmem_limit_bytes=40 * 2**20),
            name="backward",
        )(*parts)
        return solved.reshape(rows, length)

    return jnp.stack([one_field(source[f], screening[f : f + 1]) for f in range(fields)])


def solution(mesh):
    return jax.shard_map(
        on_device,
        mesh=mesh,
        in_specs=(P("af", GRID_AXES, None), P("af")),
        out_specs=P("af", GRID_AXES, None),
        check_vma=False,
    )
```

time: 22.2 us -> 16.7 us (0.75)
  Pallas kernels: 21.4 us -> 15.9 us
    pallas_call x1, Pallas kernels: 16.9 us -> 12.9 us  [one_field(): pl.pallas_call(functools.partial(forward_kernel, groups, pitch), out_shap...]
    pallas_call x1, Pallas kernels: 4.48 us -> 2.96 us  [one_field(): pl.pallas_call(functools.partial(backward_kernel, groups, pitch), out_sha...]
where the time goes in v2:
time: 16.7 us; the launch traced here: 16.5 us
  Pallas kernels  15.9 us (95%)
  between operations  0.66 us (4%)
    pallas_call x1, Pallas kernels, one_field(): pl.pallas_call(functools.partial(forward_kernel, groups, pitch), out_shap...  12.9 us
    pallas_call x1, Pallas kernels, one_field(): pl.pallas_call(functools.partial(backward_kernel, groups, pitch), out_sha...  2.96 us

profile of v2, /device:TPU:0, one launch (start us, length us, event | category | flops | bytes accessed | tf_op | source)
XLA Modules:
  0.0 16.5 jit_solution(15776235083450895604)
XLA Ops:
  0.7 12.9 %forward.1 = (bf16[1024,1024]{1,0:T(8,128)(2,1)S(1)}, bf16[1024,1024]{1,0:T(8,128)(2,1)S(1)}, f32[512,1024]{1,0:T(8,128)S(1)}, bf16[512,256]{1,0:T(8,128)(2,1)S(...) custom-call(f32[8,32,2048]{2,1,0:T(8,128)} %bitcast.2, ...), custom_call_target="tpu_custom_call" | custom-call | tf_op jit(solution)/shard_map/forward/pallas_call | solution.py:432
  13.6 3.0 %backward.1 = f32[8,32,2048]{2,1,0:T(8,128)} custom-call(bf16[1024,1024]{1,0:T(8,128)(2,1)S(1)} %get-tuple-element.15.table_high, bf16[1024,1024]{1,0:T(8,128)(2,1)S(1)} %get-tuple-element.16.table_low, f32[512,1024]{1,0:T(8,128)S(1)} %get-tuple-element.17.partial, bf16[512,256]{1,0:T(8,128)(2,1)S(1)} %get-tuple-element.18.next_high, ...), custom_call_target="tpu_custom_call" | custom-call | tf_op jit(solution)/shard_map/backward/pallas_call | solution.py:458

commit v3 on v2

--- a/solution.py
+++ b/solution.py
@@ -113,7 +113,7 @@
         coefficients[index] = value
 
 
-def boundary_states(groups, moments_of, coefficients, left_parts, right_parts, left_states, right_states):
+def boundary_states(groups, moments_of, coefficients, left_parts, right_parts, left_states, right_states, columns):
     decay, stride, block, whole, edge, scale = coefficients
     position = lax.axis_index(GRID_AXES)
     moments = [moments_of((position + groups - d) % groups) for d in range(groups)]
@@ -132,18 +132,18 @@
         right_state = block * right_state + moments[e][1:2, :]
     after_states = []
     for s in range(SEGMENTS):
-        left_states[s : s + 1, :] = left_own
-        left_own = stride * left_own + left_parts[s : s + 1, :]
+        left_states[s : s + 1, columns] = left_own
+        left_own = stride * left_own + left_parts[s : s + 1, columns]
         after_states.append(left_own)
     for s in reversed(range(SEGMENTS)):
-        right_states[s : s + 1, :] = (right_own + decay * after_states[s]) * scale
-        right_own = stride * right_own + right_parts[s : s + 1, :]
-
-
-def solve_lines(spectrum, decay, left_states, right_states, high, low):
+        right_states[s : s + 1, columns] = (right_own + decay * after_states[s]) * scale
+        right_own = stride * right_own + right_parts[s : s + 1, columns]
+
+
+def solve_lines(spectrum, decay, left_states, right_states, high, low, parts=(0, 1)):
     rows = spectrum.shape[0]
     steps = rows // SEGMENTS
-    for h in range(2):
+    for h in parts:
         columns = tile_columns(h)
         ratio = jnp.broadcast_to(decay[:, columns], (SEGMENTS, TILE))
         state = left_states[:, columns]
@@ -155,14 +155,14 @@
         for g in reversed(range(0, steps, 2)):
             later = ratio * (state + sums[g + 1])
             state = ratio * (later + sums[g])
-            place = pl.ds(h * rows + g * SEGMENTS, 2 * SEGMENTS)
+            place = pl.ds((h - parts[0]) * rows + g * SEGMENTS, 2 * SEGMENTS)
             high[place, :], low[place, :] = split(jnp.concatenate([state, later], axis=0))
 
 
-def line_sums(spectrum, decay, stride, left_parts, right_parts, moments):
+def line_sums(spectrum, decay, stride, left_parts, right_parts, moments, parts=(0, 1)):
     rows = spectrum.shape[0]
     steps = rows // SEGMENTS
-    for h in range(2):
+    for h in parts:
         columns = tile_columns(h)
         ratio = jnp.broadcast_to(decay[:, columns], (SEGMENTS, TILE))
         left = right = jnp.zeros((SEGMENTS, TILE), jnp.float32)
@@ -172,12 +172,13 @@
             right = ratio * right + spectrum[mirror * SEGMENTS : (mirror + 1) * SEGMENTS, columns]
         left_parts[:, columns] = left
         right_parts[:, columns] = right
-    left = right = jnp.zeros_like(decay)
-    for s in range(SEGMENTS):
-        left = stride * left + left_parts[s : s + 1, :]
-        right = stride * right + right_parts[SEGMENTS - 1 - s : SEGMENTS - s, :]
-    moments[0:1, :] = left
-    moments[1:2, :] = right
+        jump = stride[:, columns]
+        left = right = jnp.zeros_like(jump)
+        for s in range(SEGMENTS):
+            left = jump * left + left_parts[s : s + 1, columns]
+            right = jump * right + right_parts[SEGMENTS - 1 - s : SEGMENTS - s, columns]
+        moments[0:1, columns] = left
+        moments[1:2, columns] = right
 
 
 def forward_kernel(
@@ -185,7 +186,7 @@
     table_high, table_low, partial, next_high, next_low,
     last_spectrum, last_left, last_right, last_moments, coefficients,
     angles, angle_sems, cosines_here, cosines_sem, stage, arrived, high, low, back_high, back_low,
-    spectrum, left_parts, right_parts, left_states, right_states,
+    spectrum, left_parts, right_parts, left_states, right_states, last_left_states, last_right_states,
     landed, send_sems, recv_sems,
 ):
     _, steps, length = source.shape
@@ -248,6 +249,10 @@
         for c in chosen:
             copies[c].wait()
             copies[blocks - 1 - c].wait()
+        if begin:
+            for copy in angle_copies[1:]:
+                copy.wait()
+            pl.semaphore_wait(barrier, groups - 1)
         for c in chosen:
             columns = pl.ds(c * LANES, LANES)
             for g in range(0, steps, 2):
@@ -262,10 +267,6 @@
                 far = mirrored(load(blocks - 1 - c))
                 high[place, columns], low[place, columns] = split(near - far)
                 high[place_sum, columns], low[place_sum, columns] = split((near + far) * signs)
-    for copy in angle_copies[1:]:
-        copy.wait()
-    pl.semaphore_wait(barrier, groups - 1)
-
     def lines_of(t):
         return last_spectrum if t == last else spectrum.at[t]
 
@@ -281,23 +282,36 @@
                 high[place, :], low[place, :], table_high[:, columns], table_low[:, columns]
             )
 
-    sends = []
-
-    def sum_lines(t):
-        line_sums(lines_of(t), row_of(0, t), row_of(1, t), *sums_of(t), landed.at[t, 0])
-
-    def send(t):
+    every = (0, 1)
+    whole_tile = slice(0, 2 * TILE)
+    parcels = [(t, every, whole_tile) for t in range(last)] + [(last, (h,), tile_columns(h)) for h in every]
+
+    def sum_lines(t, parts=every):
+        line_sums(lines_of(t), row_of(0, t), row_of(1, t), *sums_of(t), landed.at[t, 0], parts)
+
+    def send(p):
+        t, _, columns = parcels[p]
         for d in range(1, groups):
-            copy = pltpu.make_async_remote_copy(
-                src_ref=landed.at[t, 0],
-                dst_ref=landed.at[t, d],
-                send_sem=send_sems.at[t, d],
-                recv_sem=recv_sems.at[t, d],
+            pltpu.make_async_remote_copy(
+                src_ref=landed.at[t, 0, :, columns],
+                dst_ref=landed.at[t, d, :, columns],
+                send_sem=send_sems.at[p],
+                recv_sem=recv_sems.at[p],
                 device_id=peer((position + d) % groups),
                 device_id_type=MESH,
-            )
-            copy.start()
-            sends.append(copy)
+            ).start()
+
+    def all_of(p):
+        t, _, columns = parcels[p]
+        ref = landed.at[t, pl.ds(1, groups - 1), :, columns]
+        return pltpu.make_async_remote_copy(
+            src_ref=ref,
+            dst_ref=ref,
+            send_sem=send_sems.at[p],
+            recv_sem=recv_sems.at[p],
+            device_id=peer((position + 1) % groups),
+            device_id_type=MESH,
+        )
 
     for t in range(tiles):
         transform(t, 0)
@@ -307,12 +321,10 @@
         transform(t, 1)
         if t < last:
             make_table(t + 1)
-    sum_lines(last)
+    sum_lines(last, (0,))
     send(last)
-
-    def receive(t):
-        for copy in sends[t * (groups - 1) : (t + 1) * (groups - 1)]:
-            copy.wait_recv()
+    sum_lines(last, (1,))
+    send(tiles)
 
     def multiply(t):
         inner = slice(t * TILE, (t + 1) * TILE)
@@ -325,23 +337,23 @@
                 )
                 partial[place, columns] = values if t == 0 else partial[place, columns] + values
 
-    if last < 2:
-        partial[...] = jnp.zeros_like(partial)
-    for t in range(last):
-        receive(t)
-        if t:
-            multiply(t - 1)
+    for p in range(tiles):
+        t, parts, columns = parcels[p]
+        all_of(p).wait_recv()
+        if p:
+            multiply(p - 1)
+        states = (last_left_states, last_right_states) if t == last else (left_states.at[t], right_states.at[t])
         boundary_states(
-            groups, lambda index, t=t: landed[t, index], [row_of(i, t) for i in range(COEFFICIENTS)],
-            left_parts.at[t], right_parts.at[t], left_states.at[t], right_states.at[t],
+            groups, lambda index: landed[t, index, :, columns], [row_of(i, t)[:, columns] for i in range(COEFFICIENTS)],
+            *sums_of(t), *states, columns,
         )
-        target = (next_high, next_low) if t == last - 1 else (back_high.at[t], back_low.at[t])
-        solve_lines(spectrum.at[t], row_of(0, t), left_states.at[t], right_states.at[t], *target)
-    receive(last)
+        target = (next_high, next_low) if t == last else (back_high.at[t], back_low.at[t])
+        solve_lines(lines_of(t), row_of(0, t), *states, *target, parts)
+    all_of(tiles).wait_recv()
     for d in range(groups):
         last_moments[d] = landed[last, d]
-    for copy in sends:
-        copy.wait_send()
+    for p in range(tiles + 1):
+        all_of(p).wait_send()
 
 
 def backward_kernel(
@@ -354,43 +366,45 @@
     half = length // 2
     blocks = length // LANES
     tiles = half // TILE
-    before = slice((tiles - 2) * TILE, (tiles - 1) * TILE)
     inner = slice((tiles - 1) * TILE, tiles * TILE)
 
-    def multiply(lines_high, lines_low, inner, n, base):
+    def multiply(lines_high, lines_low, h, n):
         columns = tile_columns(n)
         values = []
-        for h in range(2):
-            place = slice(h * rows, (h + 1) * rows)
+        for k in range(2):
+            part = slice(k * rows // 2, (k + 1) * rows // 2)
+            place = slice(h * rows + k * rows // 2, h * rows + (k + 1) * rows // 2)
             values.append(
-                base[place, columns]
-                + product(lines_high[place, :], lines_low[place, :], table_high[inner, columns], table_low[inner, columns])
+                partial[place, columns]
+                + product(lines_high[part, :], lines_low[part, :], table_high[inner, columns], table_low[inner, columns])
             )
-        return values
+        return jnp.concatenate(values, axis=0)
 
     for n in range(tiles):
-        odd, even = multiply(next_high, next_low, before, n, partial)
-        acc[:rows, tile_columns(n)] = odd
-        acc[rows:, tile_columns(n)] = even
-    row_values = [coefficients[i, tiles - 1 : tiles, :] for i in range(COEFFICIENTS)]
+        acc[:, tile_columns(n)] = multiply(next_high, next_low, 0, n)
+    columns = tile_columns(1)
+    row_values = [coefficients[i, tiles - 1 : tiles, columns] for i in range(COEFFICIENTS)]
     boundary_states(
-        groups, lambda index: last_moments[index], row_values, last_left, last_right, left_states, right_states
+        groups, lambda index: last_moments[index, :, columns], row_values,
+        last_left, last_right, left_states, right_states, columns,
     )
-    solve_lines(last_spectrum, row_values[0], left_states, right_states, last_high, last_low)
+    solve_lines(
+        last_spectrum, coefficients[0, tiles - 1 : tiles, :], left_states, right_states, last_high, last_low, (1,)
+    )
     signs = parity((SEGMENTS, LANES))
     copies = []
-    later = multiply(last_high, last_low, inner, 0, acc)
+    later = multiply(last_high, last_low, 1, 0)
     for n in range(tiles):
-        odds, evens = later
+        evens = later
         if n + 1 < tiles:
-            later = multiply(last_high, last_low, inner, n + 1, acc)
+            later = multiply(last_high, last_low, 1, n + 1)
         for c in range(TILE // LANES):
             near = n * TILE // LANES + c
             far = blocks - 1 - near
             lanes = slice(c * LANES, (c + 1) * LANES)
             for g in range(steps):
                 place = pl.ds(g, SEGMENTS, stride=pitch)
-                odd = odds[g * SEGMENTS : (g + 1) * SEGMENTS, lanes]
+                odd = acc[g * SEGMENTS : (g + 1) * SEGMENTS, near * LANES : (near + 1) * LANES]
                 even = evens[g * SEGMENTS : (g + 1) * SEGMENTS, lanes] * signs
                 stage[near, place, :] = even + odd
                 stage[far, place, :] = mirrored(even - odd)
@@ -433,7 +447,7 @@
             functools.partial(forward_kernel, groups, pitch),
             out_shape=[
                 bf16(half, half), bf16(half, half), f32(2 * rows, half),
-                bf16(2 * rows, TILE), bf16(2 * rows, TILE),
+                bf16(rows, TILE), bf16(rows, TILE),
                 f32(rows, width), f32(SEGMENTS, width), f32(SEGMENTS, width),
                 f32(groups, 2, width), f32(COEFFICIENTS, *cosines.shape),
             ],
@@ -445,11 +459,12 @@
             ]
             + staging
             + [halves(2 * rows, half)] * 2
-            + [halves(tiles - 2, 2 * rows, TILE)] * 2
+            + [halves(tiles - 1, 2 * rows, TILE)] * 2
             + [floats(tiles - 1, rows, width)]
             + [floats(tiles - 1, SEGMENTS, width)] * 4
+            + [floats(SEGMENTS, width)] * 2
             + [floats(tiles, groups, 2, width)]
-            + [pltpu.SemaphoreType.DMA((tiles, groups))] * 2,
+            + [pltpu.SemaphoreType.DMA((tiles + 1,))] * 2,
             compiler_params=pltpu.CompilerParams(
                 vmem_limit_bytes=40 * 2**20, collective_id=0, has_side_effects=True
             ),
@@ -460,8 +475,8 @@
             out_shape=f32(SEGMENTS, steps, length),
             in_specs=[vmem] * 10,
             out_specs=hbm,
-            scratch_shapes=[floats(2 * rows, half)]
-            + [halves(2 * rows, TILE)] * 2
+            scratch_shapes=[floats(rows, half)]
+            + [halves(rows, TILE)] * 2
             + [floats(SEGMENTS, width)] * 2
             + staging,
             compiler_params=pltpu.CompilerParams(vmem_limit_bytes=40 * 2**20),

time: 16.7 us -> 16.4 us (0.982)
  Pallas kernels: 15.9 us -> 15.6 us
    pallas_call x1, Pallas kernels: 2.96 us -> 2.46 us  [one_field(): pl.pallas_call(functools.partial(backward_kernel, groups, pitch), out_sha...]
    pallas_call x1, Pallas kernels: 12.9 us -> 13.1 us  [one_field(): pl.pallas_call(functools.partial(forward_kernel, groups, pitch), out_shap...]
where the time goes in v3:
time: 16.4 us; the launch traced here: 16.2 us
  Pallas kernels  15.6 us (95%)
  between operations  0.66 us (4%)
    pallas_call x1, Pallas kernels, one_field(): pl.pallas_call(functools.partial(forward_kernel, groups, pitch), out_shap...  13.1 us
    pallas_call x1, Pallas kernels, one_field(): pl.pallas_call(functools.partial(backward_kernel, groups, pitch), out_sha...  2.46 us

profile of v3, /device:TPU:0, one launch (start us, length us, event | category | flops | bytes accessed | tf_op | source)
XLA Modules:
  0.0 16.2 jit_solution(17717752260873232511)
XLA Ops:
  0.7 13.1 %forward.1 = (bf16[1024,1024]{1,0:T(8,128)(2,1)S(1)}, bf16[1024,1024]{1,0:T(8,128)(2,1)S(1)}, f32[512,1024]{1,0:T(8,128)S(1)}, bf16[256,256]{1,0:T(8,128)(2,1)S(...) custom-call(f32[8,32,2048]{2,1,0:T(8,128)} %bitcast.2, ...), custom_call_target="tpu_custom_call" | custom-call | tf_op jit(solution)/shard_map/forward/pallas_call | solution.py:446
  13.8 2.5 %backward.1 = f32[8,32,2048]{2,1,0:T(8,128)} custom-call(bf16[1024,1024]{1,0:T(8,128)(2,1)S(1)} %get-tuple-element.15.table_high, bf16[1024,1024]{1,0:T(8,128)(2,1)S(1)} %get-tuple-element.16.table_low, f32[512,1024]{1,0:T(8,128)S(1)} %get-tuple-element.17.partial, bf16[256,256]{1,0:T(8,128)(2,1)S(1)} %get-tuple-element.18.next_high, ...), custom_call_target="tpu_custom_call" | custom-call | tf_op jit(solution)/shard_map/backward/pallas_call | solution.py:473

commit v4 on v3

--- a/solution.py
+++ b/solution.py
@@ -14,6 +14,7 @@
 TILE = 256
 STEP = 32
 COEFFICIENTS = 6
+AHEAD = 2
 GRID_AXES = ("gx", "gy")
 MESH = pl.DeviceIdType.MESH
 
@@ -182,11 +183,11 @@
 
 
 def forward_kernel(
-    groups, pitch, source, screening, constants, cosines,
+    groups, pitch, early, source, screening, constants, cosines,
     table_high, table_low, partial, next_high, next_low,
     last_spectrum, last_left, last_right, last_moments, coefficients,
     angles, angle_sems, cosines_here, cosines_sem, stage, arrived, high, low, back_high, back_low,
-    spectrum, left_parts, right_parts, left_states, right_states, last_left_states, last_right_states,
+    spectrum, left_parts, right_parts, left_states, right_states,
     landed, send_sems, recv_sems,
 ):
     _, steps, length = source.shape
@@ -326,29 +327,25 @@
     sum_lines(last, (1,))
     send(tiles)
 
-    def multiply(t):
+    def multiply(t, high, low, chosen):
         inner = slice(t * TILE, (t + 1) * TILE)
-        for n in range(tiles):
+        for n in chosen:
             columns = tile_columns(n)
-            for h in range(2):
+            for h in every:
                 place = slice(h * rows, (h + 1) * rows)
-                values = product(
-                    back_high[t, place, :], back_low[t, place, :], table_high[inner, columns], table_low[inner, columns]
-                )
+                values = product(high[place, :], low[place, :], table_high[inner, columns], table_low[inner, columns])
                 partial[place, columns] = values if t == 0 else partial[place, columns] + values
 
-    for p in range(tiles):
-        t, parts, columns = parcels[p]
-        all_of(p).wait_recv()
-        if p:
-            multiply(p - 1)
-        states = (last_left_states, last_right_states) if t == last else (left_states.at[t], right_states.at[t])
+    for t in range(last):
+        all_of(t).wait_recv()
         boundary_states(
-            groups, lambda index: landed[t, index, :, columns], [row_of(i, t)[:, columns] for i in range(COEFFICIENTS)],
-            *sums_of(t), *states, columns,
+            groups, lambda index: landed[t, index], [row_of(i, t) for i in range(COEFFICIENTS)],
+            *sums_of(t), left_states.at[t], right_states.at[t], whole_tile,
         )
-        target = (next_high, next_low) if t == last else (back_high.at[t], back_low.at[t])
-        solve_lines(lines_of(t), row_of(0, t), *states, *target, parts)
+        target = (next_high, next_low) if t == last - 1 else (back_high.at[t], back_low.at[t])
+        solve_lines(lines_of(t), row_of(0, t), left_states.at[t], right_states.at[t], *target)
+        multiply(t, *target, range(early if t == last - 1 else tiles))
+    all_of(last).wait_recv()
     all_of(tiles).wait_recv()
     for d in range(groups):
         last_moments[d] = landed[last, d]
@@ -357,7 +354,7 @@
 
 
 def backward_kernel(
-    groups, pitch, table_high, table_low, partial, next_high, next_low,
+    groups, pitch, early, table_high, table_low, partial, next_high, next_low,
     last_spectrum, last_left, last_right, last_moments, coefficients,
     solved, acc, last_high, last_low, left_states, right_states, stage, stored,
 ):
@@ -366,45 +363,43 @@
     half = length // 2
     blocks = length // LANES
     tiles = half // TILE
-    inner = slice((tiles - 1) * TILE, tiles * TILE)
-
-    def multiply(lines_high, lines_low, h, n):
+    last = tiles - 1
+
+    def multiply(t, high, low, base, n):
         columns = tile_columns(n)
+        inner = slice(t * TILE, (t + 1) * TILE)
         values = []
-        for k in range(2):
-            part = slice(k * rows // 2, (k + 1) * rows // 2)
-            place = slice(h * rows + k * rows // 2, h * rows + (k + 1) * rows // 2)
+        for h in range(2):
+            place = slice(h * rows, (h + 1) * rows)
             values.append(
-                partial[place, columns]
-                + product(lines_high[part, :], lines_low[part, :], table_high[inner, columns], table_low[inner, columns])
+                base[place, columns]
+                + product(high[place, :], low[place, :], table_high[inner, columns], table_low[inner, columns])
             )
-        return jnp.concatenate(values, axis=0)
-
-    for n in range(tiles):
-        acc[:, tile_columns(n)] = multiply(next_high, next_low, 0, n)
-    columns = tile_columns(1)
-    row_values = [coefficients[i, tiles - 1 : tiles, columns] for i in range(COEFFICIENTS)]
+        return values
+
+    for n in range(early, tiles):
+        acc[:rows, tile_columns(n)], acc[rows:, tile_columns(n)] = multiply(last - 1, next_high, next_low, partial, n)
+    row_values = [coefficients[i, last:tiles, :] for i in range(COEFFICIENTS)]
     boundary_states(
-        groups, lambda index: last_moments[index, :, columns], row_values,
-        last_left, last_right, left_states, right_states, columns,
+        groups, lambda index: last_moments[index], row_values,
+        last_left, last_right, left_states, right_states, slice(0, 2 * TILE),
     )
-    solve_lines(
-        last_spectrum, coefficients[0, tiles - 1 : tiles, :], left_states, right_states, last_high, last_low, (1,)
-    )
+    solve_lines(last_spectrum, row_values[0], left_states, right_states, last_high, last_low)
     signs = parity((SEGMENTS, LANES))
     copies = []
-    later = multiply(last_high, last_low, 1, 0)
+    ready = []
     for n in range(tiles):
-        evens = later
-        if n + 1 < tiles:
-            later = multiply(last_high, last_low, 1, n + 1)
+        while len(ready) < min(n + AHEAD, tiles):
+            m = len(ready)
+            ready.append(multiply(last, last_high, last_low, partial if m < early else acc, m))
+        odds, evens = ready[n]
         for c in range(TILE // LANES):
             near = n * TILE // LANES + c
             far = blocks - 1 - near
             lanes = slice(c * LANES, (c + 1) * LANES)
             for g in range(steps):
                 place = pl.ds(g, SEGMENTS, stride=pitch)
-                odd = acc[g * SEGMENTS : (g + 1) * SEGMENTS, near * LANES : (near + 1) * LANES]
+                odd = odds[g * SEGMENTS : (g + 1) * SEGMENTS, lanes]
                 even = evens[g * SEGMENTS : (g + 1) * SEGMENTS, lanes] * signs
                 stage[near, place, :] = even + odd
                 stage[far, place, :] = mirrored(even - odd)
@@ -444,10 +439,10 @@
 
     def one_field(grid, constant):
         parts = pl.pallas_call(
-            functools.partial(forward_kernel, groups, pitch),
+            functools.partial(forward_kernel, groups, pitch, tiles // 2),
             out_shape=[
                 bf16(half, half), bf16(half, half), f32(2 * rows, half),
-                bf16(rows, TILE), bf16(rows, TILE),
+                bf16(2 * rows, TILE), bf16(2 * rows, TILE),
                 f32(rows, width), f32(SEGMENTS, width), f32(SEGMENTS, width),
                 f32(groups, 2, width), f32(COEFFICIENTS, *cosines.shape),
             ],
@@ -462,7 +457,6 @@
             + [halves(tiles - 1, 2 * rows, TILE)] * 2
             + [floats(tiles - 1, rows, width)]
             + [floats(tiles - 1, SEGMENTS, width)] * 4
-            + [floats(SEGMENTS, width)] * 2
             + [floats(tiles, groups, 2, width)]
             + [pltpu.SemaphoreType.DMA((tiles + 1,))] * 2,
             compiler_params=pltpu.CompilerParams(
@@ -471,12 +465,12 @@
             name="forward",
         )(stay(grid.reshape(SEGMENTS, steps, length)), constant, stay(constants), stay(cosines))
         solved = pl.pallas_call(
-            functools.partial(backward_kernel, groups, pitch),
+            functools.partial(backward_kernel, groups, pitch, tiles // 2),
             out_shape=f32(SEGMENTS, steps, length),
             in_specs=[vmem] * 10,
             out_specs=hbm,
-            scratch_shapes=[floats(rows, half)]
-            + [halves(rows, TILE)] * 2
+            scratch_shapes=[floats(2 * rows, half)]
+            + [halves(2 * rows, TILE)] * 2
             + [floats(SEGMENTS, width)] * 2
             + staging,
             compiler_params=pltpu.CompilerParams(vmem_limit_bytes=40 * 2**20),

time: 16.4 us -> 15.4 us (0.939)
  Pallas kernels: 15.6 us -> 14.6 us
    pallas_call x2, Pallas kernels: 15.6 us -> 14.6 us  [the longest x1 12.1 us: one_field(): pl.pallas_call(functools.partial(forward_kernel, groups, pitch, tiles //...]
where the time goes in v4:
time: 15.4 us; the launch traced here: 15.3 us
  Pallas kernels  14.6 us (95%)
  between operations  0.66 us (4%)
    pallas_call x1, Pallas kernels, one_field(): pl.pallas_call(functools.partial(forward_kernel, groups, pitch, tiles //...  12.1 us
    pallas_call x1, Pallas kernels, one_field(): pl.pallas_call(functools.partial(backward_kernel, groups, pitch, tiles //...  2.55 us

profile of v4, /device:TPU:0, one launch (start us, length us, event | category | flops | bytes accessed | tf_op | source)
XLA Modules:
  0.0 15.3 jit_solution(1359969769261950357)
XLA Ops:
  0.7 12.1 %forward.1 = (bf16[1024,1024]{1,0:T(8,128)(2,1)S(1)}, bf16[1024,1024]{1,0:T(8,128)(2,1)S(1)}, f32[512,1024]{1,0:T(8,128)S(1)}, bf16[512,256]{1,0:T(8,128)(2,1)S(...) custom-call(f32[8,32,2048]{2,1,0:T(8,128)} %bitcast.2, ...), custom_call_target="tpu_custom_call" | custom-call | tf_op jit(solution)/shard_map/forward/pallas_call | solution.py:441
  12.7 2.6 %backward.1 = f32[8,32,2048]{2,1,0:T(8,128)} custom-call(bf16[1024,1024]{1,0:T(8,128)(2,1)S(1)} %get-tuple-element.15.table_high, bf16[1024,1024]{1,0:T(8,128)(2,1)S(1)} %get-tuple-element.16.table_low, f32[512,1024]{1,0:T(8,128)S(1)} %get-tuple-element.17.partial, bf16[512,256]{1,0:T(8,128)(2,1)S(1)} %get-tuple-element.18.next_high, ...), custom_call_target="tpu_custom_call" | custom-call | tf_op jit(solution)/shard_map/backward/pallas_call | solution.py:467

commit v5 on v4

--- a/solution.py
+++ b/solution.py
@@ -274,14 +274,17 @@
     def sums_of(t):
         return (last_left, last_right) if t == last else (left_parts.at[t], right_parts.at[t])
 
-    def transform(t, h):
+    def transform(t, h, begin=0, end=2):
         columns = tile_columns(t)
+        inner = slice(begin * half // 2, end * half // 2)
         for k in range(2):
             part = slice(k * rows // 2, (k + 1) * rows // 2)
             place = slice(h * rows + k * rows // 2, h * rows + (k + 1) * rows // 2)
-            lines_of(t)[part, tile_columns(h)] = product(
-                high[place, :], low[place, :], table_high[:, columns], table_low[:, columns]
+            values = product(
+                high[place, inner], low[place, inner], table_high[inner, columns], table_low[inner, columns]
             )
+            target = lines_of(t)
+            target[part, tile_columns(h)] = target[part, tile_columns(h)] + values if begin else values
 
     every = (0, 1)
     whole_tile = slice(0, 2 * TILE)
@@ -315,14 +318,17 @@
         )
 
     for t in range(tiles):
-        transform(t, 0)
         if t:
-            sum_lines(t - 1)
+            transform(t, 0, 0, 1)
+            sum_lines(t - 1, (1,))
             send(t - 1)
+            transform(t, 0, 1, 2)
+        else:
+            transform(t, 0)
         transform(t, 1)
         if t < last:
             make_table(t + 1)
-    sum_lines(last, (0,))
+        sum_lines(t, (0,))
     send(last)
     sum_lines(last, (1,))
     send(tiles)
@@ -336,15 +342,19 @@
                 values = product(high[place, :], low[place, :], table_high[inner, columns], table_low[inner, columns])
                 partial[place, columns] = values if t == 0 else partial[place, columns] + values
 
+    def target_of(t):
+        return (next_high, next_low) if t == last - 1 else (back_high.at[t], back_low.at[t])
+
     for t in range(last):
         all_of(t).wait_recv()
+        if t:
+            multiply(t - 1, *target_of(t - 1), (tiles - 1,))
         boundary_states(
             groups, lambda index: landed[t, index], [row_of(i, t) for i in range(COEFFICIENTS)],
             *sums_of(t), left_states.at[t], right_states.at[t], whole_tile,
         )
-        target = (next_high, next_low) if t == last - 1 else (back_high.at[t], back_low.at[t])
-        solve_lines(lines_of(t), row_of(0, t), left_states.at[t], right_states.at[t], *target)
-        multiply(t, *target, range(early if t == last - 1 else tiles))
+        solve_lines(lines_of(t), row_of(0, t), left_states.at[t], right_states.at[t], *target_of(t))
+        multiply(t, *target_of(t), range(early if t == last - 1 else tiles - 1))
     all_of(last).wait_recv()
     all_of(tiles).wait_recv()
     for d in range(groups):

time: 15.4 us -> 15.5 us (level)
  no operation moved by 1% of the time
where the time goes in v5:
time: 15.5 us; the launch traced here: 15.4 us
  Pallas kernels  14.7 us (95%)
  between operations  0.66 us (4%)
    pallas_call x1, Pallas kernels, one_field(): pl.pallas_call(functools.partial(forward_kernel, groups, pitch, tiles //...  12.2 us
    pallas_call x1, Pallas kernels, one_field(): pl.pallas_call(functools.partial(backward_kernel, groups, pitch, tiles //...  2.55 us

profile of v5, /device:TPU:0, one launch (start us, length us, event | category | flops | bytes accessed | tf_op | source)
XLA Modules:
  0.0 15.4 jit_solution(15412032434996749204)
XLA Ops:
  0.7 12.2 %forward.1 = (bf16[1024,1024]{1,0:T(8,128)(2,1)S(1)}, bf16[1024,1024]{1,0:T(8,128)(2,1)S(1)}, f32[512,1024]{1,0:T(8,128)S(1)}, bf16[512,256]{1,0:T(8,128)(2,1)S(...) custom-call(f32[8,32,2048]{2,1,0:T(8,128)} %bitcast.2, ...), custom_call_target="tpu_custom_call" | custom-call | tf_op jit(solution)/shard_map/forward/pallas_call | solution.py:451
  12.8 2.6 %backward.1 = f32[8,32,2048]{2,1,0:T(8,128)} custom-call(bf16[1024,1024]{1,0:T(8,128)(2,1)S(1)} %get-tuple-element.15.table_high, bf16[1024,1024]{1,0:T(8,128)(2,1)S(1)} %get-tuple-element.16.table_low, f32[512,1024]{1,0:T(8,128)S(1)} %get-tuple-element.17.partial, bf16[512,256]{1,0:T(8,128)(2,1)S(1)} %get-tuple-element.18.next_high, ...), custom_call_target="tpu_custom_call" | custom-call | tf_op jit(solution)/shard_map/backward/pallas_call | solution.py:477

commit v6 on v4

--- a/solution.py
+++ b/solution.py
@@ -285,31 +285,28 @@
 
     every = (0, 1)
     whole_tile = slice(0, 2 * TILE)
-    parcels = [(t, every, whole_tile) for t in range(last)] + [(last, (h,), tile_columns(h)) for h in every]
-
-    def sum_lines(t, parts=every):
-        line_sums(lines_of(t), row_of(0, t), row_of(1, t), *sums_of(t), landed.at[t, 0], parts)
-
-    def send(p):
-        t, _, columns = parcels[p]
+
+    def sum_lines(t):
+        line_sums(lines_of(t), row_of(0, t), row_of(1, t), *sums_of(t), landed.at[t, 0])
+
+    def send(t):
         for d in range(1, groups):
             pltpu.make_async_remote_copy(
-                src_ref=landed.at[t, 0, :, columns],
-                dst_ref=landed.at[t, d, :, columns],
-                send_sem=send_sems.at[p],
-                recv_sem=recv_sems.at[p],
+                src_ref=landed.at[t, 0],
+                dst_ref=landed.at[t, d],
+                send_sem=send_sems.at[t],
+                recv_sem=recv_sems.at[t],
                 device_id=peer((position + d) % groups),
                 device_id_type=MESH,
             ).start()
 
-    def all_of(p):
-        t, _, columns = parcels[p]
-        ref = landed.at[t, pl.ds(1, groups - 1), :, columns]
+    def all_of(t):
+        ref = landed.at[t, pl.ds(1, groups - 1)]
         return pltpu.make_async_remote_copy(
             src_ref=ref,
             dst_ref=ref,
-            send_sem=send_sems.at[p],
-            recv_sem=recv_sems.at[p],
+            send_sem=send_sems.at[t],
+            recv_sem=recv_sems.at[t],
             device_id=peer((position + 1) % groups),
             device_id_type=MESH,
         )
@@ -322,10 +319,8 @@
         transform(t, 1)
         if t < last:
             make_table(t + 1)
-    sum_lines(last, (0,))
+    sum_lines(last)
     send(last)
-    sum_lines(last, (1,))
-    send(tiles)
 
     def multiply(t, high, low, chosen):
         inner = slice(t * TILE, (t + 1) * TILE)
@@ -336,21 +331,24 @@
                 values = product(high[place, :], low[place, :], table_high[inner, columns], table_low[inner, columns])
                 partial[place, columns] = values if t == 0 else partial[place, columns] + values
 
+    def target_of(t):
+        return (next_high, next_low) if t == last - 1 else (back_high.at[t], back_low.at[t])
+
     for t in range(last):
         all_of(t).wait_recv()
+        if t:
+            multiply(t - 1, *target_of(t - 1), (tiles - 1,))
         boundary_states(
             groups, lambda index: landed[t, index], [row_of(i, t) for i in range(COEFFICIENTS)],
             *sums_of(t), left_states.at[t], right_states.at[t], whole_tile,
         )
-        target = (next_high, next_low) if t == last - 1 else (back_high.at[t], back_low.at[t])
-        solve_lines(lines_of(t), row_of(0, t), left_states.at[t], right_states.at[t], *target)
-        multiply(t, *target, range(early if t == last - 1 else tiles))
+        solve_lines(lines_of(t), row_of(0, t), left_states.at[t], right_states.at[t], *target_of(t))
+        multiply(t, *target_of(t), range(early if t == last - 1 else tiles - 1))
     all_of(last).wait_recv()
-    all_of(tiles).wait_recv()
     for d in range(groups):
         last_moments[d] = landed[last, d]
-    for p in range(tiles + 1):
-        all_of(p).wait_send()
+    for t in range(tiles):
+        all_of(t).wait_send()
 
 
 def backward_kernel(
@@ -388,6 +386,17 @@
     signs = parity((SEGMENTS, LANES))
     copies = []
     ready = []
+
+    def store(near):
+        for index in (near, blocks - 1 - near):
+            copy = pltpu.make_async_copy(
+                stage.at[index].reshape(SEGMENTS, pitch, LANES).at[:, pl.ds(0, steps), :],
+                solved.at[:, :, pl.ds(index * LANES, LANES)],
+                stored.at[index],
+            )
+            copy.start()
+            copies.append(copy)
+
     for n in range(tiles):
         while len(ready) < min(n + AHEAD, tiles):
             m = len(ready)
@@ -404,15 +413,7 @@
                 stage[near, place, :] = even + odd
                 stage[far, place, :] = mirrored(even - odd)
         for c in range(TILE // LANES):
-            near = n * TILE // LANES + c
-            for index in (near, blocks - 1 - near):
-                copy = pltpu.make_async_copy(
-                    stage.at[index].reshape(SEGMENTS, pitch, LANES).at[:, pl.ds(0, steps), :],
-                    solved.at[:, :, pl.ds(index * LANES, LANES)],
-                    stored.at[index],
-                )
-                copy.start()
-                copies.append(copy)
+            store(n * TILE // LANES + c)
     for copy in copies:
         copy.wait()
 
@@ -458,7 +459,7 @@
             + [floats(tiles - 1, rows, width)]
             + [floats(tiles - 1, SEGMENTS, width)] * 4
             + [floats(tiles, groups, 2, width)]
-            + [pltpu.SemaphoreType.DMA((tiles + 1,))] * 2,
+            + [pltpu.SemaphoreType.DMA((tiles,))] * 2,
             compiler_params=pltpu.CompilerParams(
                 vmem_limit_bytes=40 * 2**20, collective_id=0, has_side_effects=True
             ),

time: 15.4 us -> 15.4 us (level)
  no operation moved by 1% of the time
where the time goes in v6:
time: 15.4 us; the launch traced here: 15.3 us
  Pallas kernels  14.6 us (95%)
  between operations  0.66 us (4%)
    pallas_call x1, Pallas kernels, one_field(): pl.pallas_call(functools.partial(forward_kernel, groups, pitch, tiles //...  12 us
    pallas_call x1, Pallas kernels, one_field(): pl.pallas_call(functools.partial(backward_kernel, groups, pitch, tiles //...  2.55 us

profile of v6, /device:TPU:0, one launch (start us, length us, event | category | flops | bytes accessed | tf_op | source)
XLA Modules:
  0.0 15.3 jit_solution(4093514705348646647)
XLA Ops:
  0.7 12.0 %forward.1 = (bf16[1024,1024]{1,0:T(8,128)(2,1)S(1)}, bf16[1024,1024]{1,0:T(8,128)(2,1)S(1)}, f32[512,1024]{1,0:T(8,128)S(1)}, bf16[512,256]{1,0:T(8,128)(2,1)S(...) custom-call(f32[8,32,2048]{2,1,0:T(8,128)} %bitcast.2, ...), custom_call_target="tpu_custom_call" | custom-call | tf_op jit(solution)/shard_map/forward/pallas_call | solution.py:442
  12.7 2.6 %backward.1 = f32[8,32,2048]{2,1,0:T(8,128)} custom-call(bf16[1024,1024]{1,0:T(8,128)(2,1)S(1)} %get-tuple-element.15.table_high, bf16[1024,1024]{1,0:T(8,128)(2,1)S(1)} %get-tuple-element.16.table_low, f32[512,1024]{1,0:T(8,128)S(1)} %get-tuple-element.17.partial, bf16[512,256]{1,0:T(8,128)(2,1)S(1)} %get-tuple-element.18.next_high, ...), custom_call_target="tpu_custom_call" | custom-call | tf_op jit(solution)/shard_map/backward/pallas_call | solution.py:468

commit v7 on v6

--- a/solution.py
+++ b/solution.py
@@ -15,6 +15,7 @@
 STEP = 32
 COEFFICIENTS = 6
 AHEAD = 2
+FOLDS = 4
 GRID_AXES = ("gx", "gy")
 MESH = pl.DeviceIdType.MESH
 
@@ -245,12 +246,13 @@
     make_table(0)
     signs = parity((2 * SEGMENTS, LANES))
     pairs = blocks // 2
-    for begin in range(0, pairs, pairs // 2):
-        chosen = range(begin, begin + pairs // 2)
+    size = max(pairs // FOLDS, 1)
+    for begin in range(0, pairs, size):
+        chosen = range(begin, min(begin + size, pairs))
         for c in chosen:
             copies[c].wait()
             copies[blocks - 1 - c].wait()
-        if begin:
+        if begin + size >= pairs:
             for copy in angle_copies[1:]:
                 copy.wait()
             pl.semaphore_wait(barrier, groups - 1)

time: 15.4 us -> 15.3 us (level)
  no operation moved by 1% of the time
where the time goes in v7:
time: 15.3 us; the launch traced here: 15.2 us
  Pallas kernels  14.5 us (95%)
  between operations  0.66 us (4%)
    pallas_call x1, Pallas kernels, one_field(): pl.pallas_call(functools.partial(forward_kernel, groups, pitch, tiles //...  12 us
    pallas_call x1, Pallas kernels, one_field(): pl.pallas_call(functools.partial(backward_kernel, groups, pitch, tiles //...  2.55 us

profile of v7, /device:TPU:0, one launch (start us, length us, event | category | flops | bytes accessed | tf_op | source)
XLA Modules:
  0.0 15.2 jit_solution(13509410424354629217)
XLA Ops:
  0.7 12.0 %forward.1 = (bf16[1024,1024]{1,0:T(8,128)(2,1)S(1)}, bf16[1024,1024]{1,0:T(8,128)(2,1)S(1)}, f32[512,1024]{1,0:T(8,128)S(1)}, bf16[512,256]{1,0:T(8,128)(2,1)S(...) custom-call(f32[8,32,2048]{2,1,0:T(8,128)} %bitcast.2, ...), custom_call_target="tpu_custom_call" | custom-call | tf_op jit(solution)/shard_map/forward/pallas_call | solution.py:444
  12.6 2.6 %backward.1 = f32[8,32,2048]{2,1,0:T(8,128)} custom-call(bf16[1024,1024]{1,0:T(8,128)(2,1)S(1)} %get-tuple-element.15.table_high, bf16[1024,1024]{1,0:T(8,128)(2,1)S(1)} %get-tuple-element.16.table_low, f32[512,1024]{1,0:T(8,128)S(1)} %get-tuple-element.17.partial, bf16[512,256]{1,0:T(8,128)(2,1)S(1)} %get-tuple-element.18.next_high, ...), custom_call_target="tpu_custom_call" | custom-call | tf_op jit(solution)/shard_map/backward/pallas_call | solution.py:470
